TPU v7x, 128 devices: a whole 4x4x4 slice. The times are simulated.
128 devices in a mesh: pole: 16 (over y, z_lo, core), row: 2 (over z_hi), col: 4 (over x).
Axes of the slice: x: 4, y: 4, z: 4 (z_hi: 2, z_lo: 2; z = z_hi * 2 + z_lo), core: 2. Of those that a mesh axis runs over, the one named last changes fastest.
Arguments:
- l_factor: float32 [16, 2, 6, 512, 6, 512], P('pole', None, None, 'row', None, 'col'), may hold values from -0.21875 to 0.21875
- dinv: float32 [16, 2, 6, 512, 512], P('pole', None, None, 'row', 'col'), may hold values from -8 to 8, as said below
- weights: float32 [16, 2], P('pole'), may hold values from -4 to 4
- tiles: int32 [6, 24], replicated, may hold values 0 or 1
Outputs:
- density: float32 [6, 2, 256, 6, 512], P(None, 'row', 'pole', None, 'col')
Inputs may be any that keep to these rules, and one draw needn't show every extreme that they name: Each of dinv's blocks is a symmetric complex matrix.
All inputs are finite; a program needn't handle non-finite values.
Results may differ from a plain program's by a relative error of at most 0.00012.
Values sent between devices are 32-bit elements; how exact they have to be, the bound alone decides.
A program may use at most 192 MiB of HBM per device.

v0:
```python
import jax
import jax.numpy as jnp
from jax import lax
from jax.sharding import PartitionSpec as P


def in_blocks(value, dim, size):
    before, after = (value.shape[:dim], value.shape[dim + 1 :])
    return jnp.moveaxis(value.reshape(*before, size, -1, *after), dim, 0)


def sum_at_owner(value, axis, dim):
    blocks = in_blocks(value, dim, lax.axis_size(axis))
    arrived = lax.all_to_all(blocks, axis, split_axis=0, concat_axis=0, tiled=True)
    return arrived.sum(axis=0)


def in_order(blocks, dim):
    shape = list(blocks.shape[1:])
    shape[dim] *= blocks.shape[0]
    return jnp.moveaxis(blocks, 0, dim).reshape(shape)


def sent_to_all(value, axis):
    copies = jnp.broadcast_to(value, (lax.axis_size(axis), *value.shape))
    return lax.all_to_all(copies, axis, split_axis=0, concat_axis=0, tiled=True)


def gathered_copies(value, axis, dim):
    return in_order(sent_to_all(value, axis), dim)


def cdot_t(left, right):
    dims = (((0,), (0,)), ((), ()))

    def single(first, second):
        return lax.dot_general(
            first, second, dims, precision=lax.Precision.HIGHEST, preferred_element_type=jnp.float32
        )

    real = single(left[0], right[0]) - single(left[1], right[1])
    imag = single(left[0], right[1]) + single(left[1], right[0])
    return jnp.stack([real, imag])


def weigh(values, weight):
    return weight[0] * values[0] - weight[1] * values[1]


def on_device(l_factor, dinv, weights, tiles):
    nrow = lax.axis_size("row")
    npole = lax.axis_size("pole")
    row_index = lax.axis_index("row")
    factor = l_factor[0]
    diag_inv = dinv[0]
    weight = weights[0]
    nsup = factor.shape[1]
    rows_here = factor.shape[2]
    cols_here = factor.shape[4]
    width = rows_here * nrow
    tile_rows = nsup * width // tiles.shape[1]
    expanded = jnp.repeat(tiles.reshape(nsup, nsup, -1), tile_rows, axis=2)
    local_keep = lax.dynamic_slice_in_dim(expanded, row_index * rows_here, rows_here, 2)
    keep = jnp.transpose(local_keep, (1, 2, 0)).astype(jnp.float32)
    masked = factor * keep[None, :, :, :, None]
    inverse = jnp.zeros((2, nsup, rows_here, nsup, cols_here), jnp.float32)
    inverse = inverse.at[:, nsup - 1, :, nsup - 1, :].set(diag_inv[:, nsup - 1])
    for step in range(nsup - 2, -1, -1):
        span = nsup - 1 - step
        panel = lax.all_gather(masked[:, step + 1 :, :, step, :], "col", axis=3, tiled=True)
        panel_rows = panel.reshape(2, span * rows_here, width)
        block = inverse[:, step + 1 :, :, step + 1 :, :].reshape(
            2, span * rows_here, span * cols_here
        )
        partial_value = -cdot_t(panel_rows, block)
        row_mine = sum_at_owner(partial_value, "row", 1)
        row_full = gathered_copies(row_mine, "row", 1)
        inverse = inverse.at[:, step, :, step + 1 :, :].set(
            row_mine.reshape(2, rows_here, span, cols_here)
        )
        swapped = lax.all_to_all(
            row_full.reshape(2, width, span, cols_here),
            "col",
            split_axis=1,
            concat_axis=3,
            tiled=True,
        )
        mine = lax.dynamic_slice_in_dim(swapped, row_index * rows_here, rows_here, 3)
        column = jnp.transpose(mine, (0, 2, 3, 1))
        inverse = inverse.at[:, step + 1 :, :, step, :].set(column)
        correction = cdot_t(panel_rows, column.reshape(2, span * rows_here, cols_here))
        diag_share = sum_at_owner(correction, "row", 1)
        inverse = inverse.at[:, step, :, step, :].set(diag_inv[:, step] - diag_share)
    summed = lax.psum_scatter(weigh(inverse, weight), "pole", scatter_dimension=1, tiled=True)
    return summed.reshape(nsup, 1, rows_here // npole, nsup, cols_here)


def solution(mesh):
    return jax.shard_map(
        on_device,
        mesh=mesh,
        in_specs=(
            P("pole", None, None, "row", None, "col"),
            P("pole", None, None, "row", "col"),
            P("pole", None),
            P(),
        ),
        out_specs=P(None, "row", "pole", None, "col"),
        check_vma=False,
    )
```

profile of v0, /device:TPU:6, one launch (start us, length us, event | category | flops | bytes accessed | tf_op | source)
XLA Modules:
  0.0 716.6 jit_solution(17790446587292118163)
XLA Ops:
  7.6 9.7 %copy.183 = f32[1,2,6,256,6,128]{3,5,2,4,1,0:T(8,128)} copy(f32[1,2,6,256,6,128]{5,3,4,2,1,0:T(8,128)} %param.36) | data formatting | bytes 18874368 | tf_op args[0]
  29.9 21.9 %all-gather.11.cloned.1.call-done = f32[2,1,256,1,512]{2,4,1,3,0:T(8,128)} async-done(((f32[2,1,256,1,128]{2,4,1,3,0:T(8,128)}), f32[2,1,256,1,512]{2,4,1,3,0:T(8,128)}) %all-gather.11.cloned.1.call-update) | async-done | bytes 1048592 | tf_op jit(solution)/shard_map/all_gather | solution.py:70
  56.4 12.3 %all_to_all.165 = f32[2,2,256,128]{3,2,1,0:T(8,128)S(1)} all-to-all(f32[2,2,256,128]{3,2,1,0:T(8,128)S(1)} %fusion.142), channel_id=1, replica_groups=mesh['pole'=16,'row'=2,'col'=4] {'row'}, dimensions={0} | all-to-all | bytes 1048576 | tf_op jit(solution)/shard_map/all_to_all | solution.py:14
  68.7 10.5 %all_to_all.166 = f32[2,2,256,128]{3,2,1,0:T(8,128)S(1)} all-to-all(f32[2,2,256,128]{3,2,1,0:T(8,128)S(1)} %broadcast_in_dim.21), channel_id=1, replica_groups=mesh['pole'=16,'row'=2,'col'=4] {'row'}, dimensions={0} | all-to-all | bytes 1048576 | tf_op jit(solution)/shard_map/all_to_all | solution.py:26
  80.5 5.1 all-to-all-start.2
  103.1 6.6 all-to-all-done.3
  124.6 13.3 %all_to_all.167 = f32[2,2,256,256]{3,2,1,0:T(8,128)S(1)} all-to-all(f32[2,2,256,256]{3,2,1,0:T(8,128)S(1)} %fusion.127), channel_id=1, replica_groups=mesh['pole'=16,'row'=2,'col'=4] {'row'}, dimensions={0} | all-to-all | bytes 2097152 | tf_op jit(solution)/shard_map/all_to_all | solution.py:14
  145.1 8.5 %all-to-all-done.5 = f32[2,2,256,256]{3,2,1,0:T(8,128)S(1)} async-done(((f32[2,2,256,256]{3,2,1,0:T(8,128)}), f32[2,2,256,256]{3,2,1,0:T(8,128)S(1)}, u32[]{:S(2)}, u32[]{:S(2)}) %all-to-all-start.5) | async-done | bytes 1048608 | tf_op jit(solution)/shard_map/all_to_all | solution.py:26
  162.9 20.2 %all-to-all-done.6 = f32[2,512,2,128]{3,2,0,1:T(2,128)S(1)} async-done(((f32[2,512,2,128]{3,2,0,1:T(2,128)}), f32[2,512,2,128]{3,2,0,1:T(2,128)S(1)}, u32[]{:S(2)}, u32[]{:S(2)}) %all-to-all-start.6) | async-done | bytes 1048608 | tf_op jit(solution)/shard_map/all_to_all | solution.py:81
  191.3 13.0 %all-to-all-start.7 = ((f32[2,2,256,128]{3,2,1,0:T(8,128)}), f32[2,2,256,128]{3,2,1,0:T(8,128)}, u32[]{:S(2)}, u32[]{:S(2)}) async-start(f32[2,2,256,128]{3,2,1,0:T(8,128)} %maximum_bitcast_fusion.1), calls=%async_computation.7 | async-start | bytes 1048576 | tf_op jit(solution)/shard_map/all_to_all | solution.py:14
  229.6 24.9 %all_to_all.168 = f32[2,2,256,384]{3,2,1,0:T(8,128)S(1)} all-to-all(f32[2,2,256,384]{3,2,1,0:T(8,128)S(1)} %fusion.44), channel_id=1, replica_groups=mesh['pole'=16,'row'=2,'col'=4] {'row'}, dimensions={0} | all-to-all | bytes 3145728 | tf_op jit(solution)/shard_map/all_to_all | solution.py:14
  255.0 16.2 %all_to_all.169 = f32[2,2,256,384]{2,3,1,0:T(8,128)S(1)} all-to-all(f32[2,2,256,384]{2,3,1,0:T(8,128)S(1)} %broadcast_in_dim.23), channel_id=1, replica_groups=mesh['pole'=16,'row'=2,'col'=4] {'row'}, dimensions={0} | all-to-all | bytes 3145728 | tf_op jit(solution)/shard_map/all_to_all | solution.py:26
  278.6 5.5 all-to-all-start.10
  315.9 7.1 all-to-all-done.11
  345.2 28.7 %all_to_all.170 = f32[2,2,256,512]{3,2,1,0:T(8,128)S(1)} all-to-all(f32[2,2,256,512]{3,2,1,0:T(8,128)S(1)} %fusion.31), channel_id=1, replica_groups=mesh['pole'=16,'row'=2,'col'=4] {'row'}, dimensions={0} | all-to-all | bytes 4194304 | tf_op jit(solution)/shard_map/all_to_all | solution.py:14
  374.5 19.1 %all_to_all.171 = f32[2,2,256,512]{3,2,1,0:T(8,128)S(1)} all-to-all(f32[2,2,256,512]{3,2,1,0:T(8,128)S(1)} %broadcast_in_dim.24), channel_id=1, replica_groups=mesh['pole'=16,'row'=2,'col'=4] {'row'}, dimensions={0} | all-to-all | bytes 4194304 | tf_op jit(solution)/shard_map/all_to_all | solution.py:26
  398.3 7.1 all-to-all-start.14
  405.3 5.2 fusion.181
  448.1 5.7 all-to-all-done.15
  462.9 6.7 fusion.2
  469.6 7.2 %fusion.4 = f32[512,640]{1,0:T(8,128)S(1)} fusion(f32[1280,512]{1,0:T(8,128)S(1)} %bitcast.482, f32[160,8,5,128]{3,2,1,0:T(8,128)S(1)} %bitcast.479), kind=kOutput, calls=%fused_computation.7 | convolution fusion | flops 5033164800 | bytes 7208960 | tf_op jit(solution)/shard_map/dot_general | solution.py:37
  476.8 7.1 fusion.56
  483.9 6.9 fusion.53
  491.0 33.4 %all_to_all.172 = f32[2,2,256,640]{3,2,1,0:T(8,128)S(1)} all-to-all(f32[2,2,256,640]{3,2,1,0:T(8,128)S(1)} %fusion.10), channel_id=1, replica_groups=mesh['pole'=16,'row'=2,'col'=4] {'row'}, dimensions={0} | all-to-all | bytes 5242880 | tf_op jit(solution)/shard_map/all_to_all | solution.py:14
  527.7 21.9 %all_to_all.173 = f32[2,2,256,640]{2,3,1,0:T(8,128)S(1)} all-to-all(f32[2,2,256,640]{2,3,1,0:T(8,128)S(1)} %broadcast_in_dim.25), channel_id=1, replica_groups=mesh['pole'=16,'row'=2,'col'=4] {'row'}, dimensions={0} | all-to-all | bytes 5242880 | tf_op jit(solution)/shard_map/all_to_all | solution.py:26
  557.9 5.2 copy.259
  563.1 5.1 all-to-all-start.18
  575.1 10.5 %all-to-all-done.18 = f32[2,512,5,128]{3,0,2,1:T(2,128)} async-done(((f32[2,512,5,128]{3,0,2,1:T(2,128)}), f32[2,512,5,128]{3,0,2,1:T(2,128)}, u32[]{:S(2)}, u32[]{:S(2)}) %all-to-all-start.18) | async-done | bytes 2621472 | tf_op jit(solution)/shard_map/all_to_all | solution.py:81
  612.2 6.6 all-to-all-done.19
  620.5 5.8 fusion.1
  626.3 5.5 copy.266
  631.8 75.7 %reduce-scatter.2.cloned.1.call-done = f32[6,16,6,128]{3,2,0,1:T(8,128)} async-done(((f32[6,256,6,128]{3,2,0,1:T(8,128)}), f32[6,16,6,128]{3,2,0,1:T(8,128)}) %reduce-scatter.2.cloned.1.call-update) | async-done | bytes 294928 | tf_op jit(solution)/shard_map/reduce_scatter | solution.py:94
  (211 shorter events, 263.7 us)
Async XLA Ops:
  6.5 45.3 %all-gather.11.cloned.1.call-start = ((), (), s32[]{:S(2)}) async-start(), calls=%async_computation.22 | async-start | bytes 1310720 | tf_op jit(solution)/shard_map/all_gather | solution.py:70
  22.0 3.7 copy-start.3
  26.4 86.1 %all-gather.13.cloned.1.call-start = ((), (), s32[]{:S(2)}) async-start(), calls=%async_computation.23 | async-start | bytes 2621440 | tf_op jit(solution)/shard_map/all_gather | solution.py:70
  29.9 79.8 %copy-start.9 = (f32[1,2,6,256,128]{4,3,1,2,0:T(8,128)}, f32[1,2,6,256,128]{4,3,1,2,0:T(8,128)S(1)}, u32[]{:S(2)}) copy-start(f32[1,2,6,256,128]{4,3,1,2,0:T(8,128)S(1)} %copy.367) | copy-start | bytes 4718596
  51.8 3.3 copy-start.7
  80.5 12.1 %all-to-all-start.2 = ((f32[2,512,1,128]{3,0,2,1:T(2,128)}), f32[2,512,1,128]{3,0,2,1:T(2,128)S(1)}, u32[]{:S(2)}, u32[]{:S(2)}) async-start(f32[2,512,1,128]{3,0,2,1:T(2,128)} %copy.190), calls=%async_computation.2 | async-start | bytes 1048576 | tf_op jit(solution)/shard_map/all_to_all | solution.py:81
  85.6 118.6 %all-gather.15.cloned.1.call-start = ((), (), s32[]{:S(2)}) async-start(), calls=%async_computation.24 | async-start | bytes 3932160 | tf_op jit(solution)/shard_map/all_gather | solution.py:70
  97.9 11.8 %all-to-all-start.3 = ((f32[2,2,256,128]{3,2,1,0:T(8,128)}), f32[2,2,256,128]{3,2,1,0:T(8,128)S(1)}, u32[]{:S(2)}, u32[]{:S(2)}) async-start(f32[2,2,256,128]{3,2,1,0:T(8,128)} %maximum_bitcast_fusion), calls=%async_computation.3 | async-start | bytes 1048576 | tf_op jit(solution)/shard_map/all_to_all | solution.py:14
  139.1 14.5 %all-to-all-start.5 = ((f32[2,2,256,256]{3,2,1,0:T(8,128)}), f32[2,2,256,256]{3,2,1,0:T(8,128)S(1)}, u32[]{:S(2)}, u32[]{:S(2)}) async-start(f32[2,2,256,256]{3,2,1,0:T(8,128)} %broadcast_in_dim.22), calls=%async_computation.5 | async-start | bytes 2097152 | tf_op jit(solution)/shard_map/all_to_all | solution.py:26
  142.7 145.1 %all-gather.17.cloned.1.call-start = ((), (), s32[]{:S(2)}) async-start(), calls=%async_computation.25 | async-start | bytes 5242880 | tf_op jit(solution)/shard_map/all_gather | solution.py:70
  156.6 26.5 %all-to-all-start.6 = ((f32[2,512,2,128]{3,2,0,1:T(2,128)}), f32[2,512,2,128]{3,2,0,1:T(2,128)S(1)}, u32[]{:S(2)}, u32[]{:S(2)}) async-start(f32[2,512,2,128]{3,2,0,1:T(2,128)} %reshape.1057), calls=%async_computation.6 | async-start | bytes 2097152 | tf_op jit(solution)/shard_map/all_to_all | solution.py:81
  183.2 3.2 copy-start.4
  191.3 20.9 %all-to-all-start.7 = ((f32[2,2,256,128]{3,2,1,0:T(8,128)}), f32[2,2,256,128]{3,2,1,0:T(8,128)}, u32[]{:S(2)}, u32[]{:S(2)}) async-start(f32[2,2,256,128]{3,2,1,0:T(8,128)} %maximum_bitcast_fusion.1), calls=%async_computation.7 | async-start | bytes 1048576 | tf_op jit(solution)/shard_map/all_to_all | solution.py:14
  278.6 18.1 %all-to-all-start.10 = ((f32[2,512,3,128]{3,0,2,1:T(2,128)}), f32[2,512,3,128]{3,0,2,1:T(2,128)}, u32[]{:S(2)}, u32[]{:S(2)}) async-start(f32[2,512,3,128]{3,0,2,1:T(2,128)} %copy.224), calls=%async_computation.10 | async-start | bytes 3145728 | tf_op jit(solution)/shard_map/all_to_all | solution.py:81
  284.1 121.2 %all-gather.19.cloned.1.call-start = ((), (), s32[]{:S(2)}) async-start(), calls=%async_computation.26 | async-start | bytes 6553600 | tf_op jit(solution)/shard_map/all_gather | solution.py:70
  299.5 5.3 copy-start.1
  310.4 4.5 copy-start.10
  311.3 11.7 %all-to-all-start.11 = ((f32[2,2,256,128]{3,2,1,0:T(8,128)}), f32[2,2,256,128]{3,2,1,0:T(8,128)S(1)}, u32[]{:S(2)}, u32[]{:S(2)}) async-start(f32[2,2,256,128]{3,2,1,0:T(8,128)} %maximum_bitcast_fusion.2), calls=%async_computation.11 | async-start | bytes 1048576 | tf_op jit(solution)/shard_map/all_to_all | solution.py:14
  328.7 1.6 copy-start.5
  330.3 3.6 copy-start.6
  374.2 19.3 %copy-start.8 = (f32[2,256,512]{2,1,0:T(8,128)}, f32[2,256,512]{2,1,0:T(8,128)S(1)}, u32[]{:S(2)}) copy-start(f32[2,256,512]{2,1,0:T(8,128)S(1)} %reduce_sum.109) | copy-start | bytes 3145732
  398.3 25.2 %all-to-all-start.14 = ((f32[2,512,4,128]{3,2,0,1:T(4,128)}), f32[2,512,4,128]{3,2,0,1:T(4,128)}, u32[]{:S(2)}, u32[]{:S(2)}) async-start(f32[2,512,4,128]{3,2,0,1:T(4,128)} %reshape.1058), calls=%async_computation.14 | async-start | bytes 4194304 | tf_op jit(solution)/shard_map/all_to_all | solution.py:81
  429.8 6.0 copy-start
  442.0 11.7 %all-to-all-start.15 = ((f32[2,2,256,128]{3,2,1,0:T(8,128)}), f32[2,2,256,128]{3,2,1,0:T(8,128)S(1)}, u32[]{:S(2)}, u32[]{:S(2)}) async-start(f32[2,2,256,128]{3,2,1,0:T(8,128)} %maximum_bitcast_fusion.3), calls=%async_computation.15 | async-start | bytes 1048576 | tf_op jit(solution)/shard_map/all_to_all | solution.py:14
  460.9 2.0 copy-start.2
  563.1 6.5 copy-start.11
  563.1 7.1 copy-start.12
  563.1 22.5 %all-to-all-start.18 = ((f32[2,512,5,128]{3,0,2,1:T(2,128)}), f32[2,512,5,128]{3,0,2,1:T(2,128)}, u32[]{:S(2)}, u32[]{:S(2)}) async-start(f32[2,512,5,128]{3,0,2,1:T(2,128)} %copy.259), calls=%async_computation.18 | async-start | bytes 5242880 | tf_op jit(solution)/shard_map/all_to_all | solution.py:81
  589.0 12.9 %slice-start = ((s8[5242880]{0:T(1024)(128)(4,1)}), s8[1048576]{0:T(1024)(128)(4,1)S(1)}, s32[]{:S(2)}) async-start(s8[5242880]{0:T(1024)(128)(4,1)} %bitcast.476), calls=%async_computation.27 | async-start | bytes 2097152
  592.3 9.6 %slice-start.1 = ((s8[5242880]{0:T(1024)(128)(4,1)}), s8[4194304]{0:T(1024)(128)(4,1)S(1)}, s32[]{:S(2)}) async-start(s8[5242880]{0:T(1024)(128)(4,1)} %bitcast.476), calls=%async_computation.28 | async-start | bytes 8388608
  607.2 11.6 %all-to-all-start.19 = ((f32[2,2,256,128]{3,2,1,0:T(8,128)}), f32[2,2,256,128]{3,2,1,0:T(8,128)S(1)}, u32[]{:S(2)}, u32[]{:S(2)}) async-start(f32[2,2,256,128]{3,2,1,0:T(8,128)} %maximum_bitcast_fusion.4), calls=%async_computation.19 | async-start | bytes 1048576 | tf_op jit(solution)/shard_map/all_to_all | solution.py:14
  610.7 96.8 %reduce-scatter.2.cloned.1.call-start = ((), (), s32[]{:S(2)}) async-start(), calls=%async_computation.21 | async-start | bytes 6684672 | tf_op jit(solution)/shard_map/reduce_scatter | solution.py:94
Sparse Core Ops, SparseCore 0:
  26.5 25.2 all-gather.10
  53.5 31.0 all-gather.12
  88.1 39.3 all-gather.14
  145.2 57.1 all-gather.16
  286.7 54.5 all-gather.18
  631.9 75.5 reduce-scatter.1
where the time goes:
time: 728 us; the launch traced here: 717 us
  blocking collectives  180 us (25%)
  local copies, waits for them, and re-layouts  170 us (23%)
  waiting for transfers between devices  163 us (22%)
  matrix products  98.3 us (14%)
  starting transfers between devices  59.5 us (8%)
  other arithmetic  30.5 us (4%)
  between operations  14.8 us (2%)
    all_to_all x5, blocking collectives, sum_at_owner(): lax.all_to_all(blocks, axis, split_axis=0, concat_axis=0, tiled=True)  113 us
    dot_general x40, matrix products, single(): lax.dot_general(first, second, dims, precision=lax.Precision.HIGHEST, pre...  98.3 us
    reduce_scatter x1, waiting for transfers between devices, on_device(): lax.psum_scatter(weigh(inverse, weight), 'pole', scatter_dimension=1, til...  75.7 us
    all_to_all x4, blocking collectives, sent_to_all(): return lax.all_to_all(copies, axis, split_axis=0, concat_axis=0, tiled=True)  67.7 us
    slice x24, local copies, waits for them, and re-layouts, cdot_t(): real = single(left[0], right[0]) - single(left[1], right[1])  48 us
    all_to_all x5, waiting for transfers between devices, on_device(): lax.all_to_all(row_full.reshape(2, width, span, cols_here), 'col', split_...  30.7 us
    all_to_all x5, starting transfers between devices, on_device(): lax.all_to_all(row_full.reshape(2, width, span, cols_here), 'col', split_...  28 us
    all_to_all x5, starting transfers between devices, sum_at_owner(): lax.all_to_all(blocks, axis, split_axis=0, concat_axis=0, tiled=True)  27.5 us
  transfers between devices with their start and end apart: 17, of which 10 were waited for; matrix products, arithmetic and copies ran while one was open for 24% of the time, Pallas kernels for 0%

commit v1 on v0

v1 whole, which is shorter than its diff:
```python
import functools

import jax
import jax.numpy as jnp
from jax import lax
from jax.experimental import pallas as pl
from jax.experimental.pallas import tpu as pltpu
from jax.sharding import Mesh
from jax.sharding import PartitionSpec as P

AXES = ("a", "b", "zl", "core", "zh", "x")
MESH = pl.DeviceIdType.MESH


def block_order(nsup):
    lower = [("L", row, col) for col in range(1, nsup - 1) for row in range(col + 1, nsup)]
    diag = [("D", col, col) for col in range(nsup - 1, 0, -1)]
    first = [("L", row, 0) for row in range(1, nsup)]
    return lower + diag + first + [("D", 0, 0)]


def gather_kernel(nb, pack, full, z_send, z_recv, x_send, x_recv, c_send, c_recv):
    zl, core, zh, x = (lax.axis_index(n) for n in ("zl", "core", "zh", "x"))
    ncol = lax.axis_size("x")
    right, left = lax.rem(x + 1, ncol), lax.rem(x + ncol - 1, ncol)
    far = lax.rem(x + 2, ncol)
    to_z = {"zl": 1 - zl, "core": zh, "zh": core}
    to_right, to_left, to_core = {"x": right}, {"x": left}, {"core": 1 - core}
    rows, cols = pack.shape[2], pack.shape[3]

    barrier = pltpu.get_barrier_semaphore()
    for peer in (to_z, to_right, to_left, to_core):
        pl.semaphore_signal(barrier, inc=1, device_id=peer, device_id_type=MESH)
    pl.semaphore_wait(barrier, 4)

    def tile(b, row, col, parts=pl.ds(0, 2)):
        return full.at[
            b,
            parts,
            pl.ds(pl.multiple_of(row * rows, rows), rows),
            pl.ds(pl.multiple_of(col * cols, cols), cols),
        ]

    def z_copy(b):
        return pltpu.make_async_remote_copy(
            pack.at[b], tile(b, zh, x), z_send.at[b], z_recv.at[b], device_id=to_z, device_id_type=MESH
        )

    def z_wait(b):
        pltpu.make_async_remote_copy(
            pack.at[b], tile(b, core, x), z_send.at[b], z_recv.at[b], device_id=to_z, device_id_type=MESH
        ).wait_recv()

    half = (pl.ds(0, 1), pl.ds(1, 1))

    def x_copy(b, kind, col, parts, peer):
        ref = tile(b, core, col, parts)
        return pltpu.make_async_remote_copy(
            ref, ref, x_send.at[kind, b], x_recv.at[kind, b], device_id=peer, device_id_type=MESH
        )

    def c_copy(b, kind, col, parts=pl.ds(0, 2), row=None):
        ref = tile(b, core if row is None else row, col, parts)
        return pltpu.make_async_remote_copy(
            ref, ref, c_send.at[kind, b], c_recv.at[kind, b], device_id=to_core, device_id_type=MESH
        )

    both = pl.ds(0, 2)
    last = nb - 1

    @pl.loop(0, nb)
    def _(b):
        z_copy(b).start()

    def own(b):
        z_wait(b)
        x_copy(b, 0, x, both, to_right).start()
        x_copy(b, 1, x, both, to_left).start()
        c_copy(b, 0, x).start()

    def pass_on(b):
        x_copy(b, 0, left, both, to_right).wait_recv()
        x_copy(b, 2, left, half[0], to_right).start()
        c_copy(b, 1, left).start()
        x_copy(b, 1, right, both, to_left).wait_recv()
        x_copy(b, 3, right, half[1], to_left).start()
        c_copy(b, 2, right).start()

    def finish(b):
        x_copy(b, 2, far, half[0], to_right).wait_recv()
        c_copy(b, 3, far, half[0]).start()
        x_copy(b, 3, far, half[1], to_left).wait_recv()
        c_copy(b, 4, far, half[1]).start()

    own(0)
    own(1)
    pass_on(0)

    @pl.loop(2, last)
    def _(b):
        own(b)
        pass_on(b - 1)
        finish(b - 2)

    pass_on(last - 1)
    z_wait(last)
    c_copy(last, 0, x).start()
    finish(last - 2)
    finish(last - 1)

    @pl.loop(0, last)
    def _(b):
        z_copy(b).wait_send()
        x_copy(b, 0, x, both, to_right).wait_send()
        x_copy(b, 1, x, both, to_left).wait_send()
        x_copy(b, 2, left, half[0], to_right).wait_send()
        x_copy(b, 3, right, half[1], to_left).wait_send()
        for kind, col, parts in ((0, x, both), (1, left, both), (2, right, both), (3, far, half[0]), (4, far, half[1])):
            c_copy(b, kind, col, parts).wait_send()
            c_copy(b, kind, col, parts, 1 - core).wait_recv()

    z_copy(last).wait_send()
    c_copy(last, 0, x).wait_send()
    c_copy(last, 0, x, both, 1 - core).wait_recv()


def gather_blocks(pack, ncol):
    nb, parts, rows, cols = pack.shape
    sems = pltpu.SemaphoreType.DMA
    return pl.pallas_call(
        functools.partial(gather_kernel, nb),
        out_shape=jax.ShapeDtypeStruct((nb, parts, 2 * rows, ncol * cols), jnp.float32),
        in_specs=[pl.BlockSpec(memory_space=pl.ANY)],
        out_specs=pl.BlockSpec(memory_space=pl.ANY),
        scratch_shapes=[sems((nb,)), sems((nb,)), sems((4, nb)), sems((4, nb)), sems((5, nb)), sems((5, nb))],
        compiler_params=pltpu.CompilerParams(collective_id=0, has_side_effects=True),
    )(pack)


def product(left, right, contract):
    def single(a, b):
        return lax.dot_general(
            a, b, (((contract,), (0,)), ((), ())), precision=lax.Precision.HIGH, preferred_element_type=jnp.float32
        )

    n = right[0].shape[1]
    both = jnp.concatenate(right, axis=1)
    by_real, by_imag = single(left[0], both), single(left[1], both)
    return by_real[:, :n] - by_imag[:, n:], by_real[:, n:] + by_imag[:, :n]


def minus(first, second):
    return first[0] - second[0], first[1] - second[1]


def on_device(l_factor, dinv, weights, tiles):
    zl, core, zh, x = (lax.axis_index(n) for n in ("zl", "core", "zh", "x"))
    ncol = lax.axis_size("x")
    factor, diag_inv = l_factor[0], dinv[0]
    nsup, rows, cols = factor.shape[1], factor.shape[2], factor.shape[4]
    width = 2 * rows
    tile_rows = nsup * width // tiles.shape[1]
    expanded = jnp.repeat(tiles.reshape(nsup, nsup, -1), tile_rows, axis=2)
    keep = lax.dynamic_slice_in_dim(expanded, zh * rows, rows, 2).astype(jnp.float32)

    order = block_order(nsup)
    where = {item: i for i, item in enumerate(order)}
    pack = jnp.stack(
        [
            factor[:, row, :, col, :] * keep[col, row][None, :, None] if kind == "L" else diag_inv[:, row]
            for kind, row, col in order
        ]
    )
    perm = [
        ((l * 2 + k) * 2 + h, ((1 - l) * 2 + h) * 2 + k) for l in range(2) for k in range(2) for h in range(2)
    ]
    weight = lax.ppermute(weights[0], ("zl", "core", "zh"), perm)
    full = gather_blocks(pack, ncol)

    n = cols // 2
    start = x * cols + core * n

    def block(kind, row, col):
        both = full[where[(kind, row, col)]]
        return both[0], both[1]

    def mine(kind, row, col):
        both = lax.dynamic_slice_in_dim(full[where[(kind, row, col)]], start, n, 2)
        return both[0], both[1]

    z = {}
    for row in range(1, nsup):
        pieces = [mine("L", row, col) for col in range(row)]
        total = tuple(jnp.concatenate([p[i] for p in pieces], axis=1) for i in range(2))
        for mid in range(1, row):
            term = product(block("L", row, mid), z[mid], 1)
            total = tuple(
                jnp.concatenate([t[:, : mid * n] - m, t[:, mid * n :]], axis=1) for t, m in zip(total, term)
            )
        z[row] = total
    h = {}
    for row in range(nsup - 1, -1, -1):
        own = mine("D", row, row)
        if row > 0:
            t = product(block("D", row, row), z[row], 1)
            own = tuple(jnp.concatenate([-t[i], own[i]], axis=1) for i in range(2))
        if row < nsup - 1:
            left = tuple(
                jnp.concatenate([block("L", low, row)[i] for low in range(row + 1, nsup)], axis=0) for i in range(2)
            )
            right = tuple(
                jnp.concatenate([h[low][i][:, : (row + 1) * n] for low in range(row + 1, nsup)], axis=0)
                for i in range(2)
            )
            own = minus(own, product(left, right, 0))
        h[row] = own
    pairs = [(row, col) for row in range(nsup) for col in range(row + 1)]
    partial_sum = jnp.concatenate([weight[0] * h[row][0] - weight[1] * h[row][1] for row in range(nsup)], axis=1)
    share = lax.psum_scatter(partial_sum, ("zh", "a", "b", "zl"), scatter_dimension=0, tiled=True)
    share = share.reshape(share.shape[0], len(pairs), n)

    low = lax.all_to_all(share, "core", split_axis=0, concat_axis=2, tiled=True)
    off = jnp.stack([share[:, i] for i, (row, col) in enumerate(pairs) if row > col], axis=0)
    swapped = lax.all_to_all(off, ("b", "zl"), split_axis=2, concat_axis=1, tiled=True)
    sizes = [lax.axis_size(name) for name in AXES]
    jumps = []
    for a in range(2):
        for b in range(2):
            for l in range(2):
                for k in range(2):
                    for h_ in range(2):
                        for c in range(ncol):
                            src = ((((a * 2 + b) * 2 + l) * 2 + k) * 2 + h_) * ncol + c
                            d = (c % 2, k, b, l, c // 2, h_ * 2 + a)
                            dst = ((((d[0] * 2 + d[1]) * 2 + d[2]) * 2 + d[3]) * 2 + d[4]) * ncol + d[5]
                            jumps.append((src, dst))
    mirrored = jnp.swapaxes(lax.ppermute(swapped, AXES, jumps), 1, 2)

    spot = {pair: i for i, pair in enumerate(pairs)}
    offs = {pair: i for i, pair in enumerate(p for p in pairs if p[0] > p[1])}
    grid = [
        jnp.stack([low[:, spot[(row, col)]] if row >= col else mirrored[offs[(col, row)]] for col in range(nsup)], axis=1)
        for row in range(nsup)
    ]
    return jnp.stack(grid)[:, None]


def solution(mesh):
    fine = Mesh(mesh.devices.reshape(2, 2, 2, 2, 2, 4), AXES)
    pole = ("a", "b", "zl", "core")
    return jax.shard_map(
        on_device,
        mesh=fine,
        in_specs=(P(pole, None, None, "zh", None, "x"), P(pole, None, None, "zh", "x"), P(pole, None), P()),
        out_specs=P(None, "zh", pole, None, "x"),
        check_vma=False,
    )
```

time: 728 us -> 538 us (0.74)
  Pallas kernels: 0 us -> 184 us
  blocking collectives: 180 us -> 3.85 us
  local copies, waits for them, and re-layouts: 170 us -> 92.6 us
  waiting for transfers between devices: 163 us -> 96.6 us
  starting transfers between devices: 59.5 us -> 9.91 us
    pallas_call x0 -> x1, Pallas kernels: none -> 184 us  [gather_blocks(): pl.pallas_call(functools.partial(gather_kernel, nb), out_shape=jax.ShapeD...]
    all_to_all x9 -> x1, blocking collectives: 180 us -> 3.85 us  [on_device(): low = lax.all_to_all(share, 'core', split_axis=0, concat_axis=2, tiled=True)]
    all_to_all x11 -> x1, waiting for transfers between devices: 65.5 us -> 2.59 us  [on_device(): lax.all_to_all(off, ('b', 'zl'), split_axis=2, concat_axis=1, tiled=True)]
    all_to_all x11 -> x1, starting transfers between devices: 59.1 us -> 3.32 us  [on_device(): lax.all_to_all(off, ('b', 'zl'), split_axis=2, concat_axis=1, tiled=True)]
    another operation x23 -> x6, local copies, waits for them, and re-layouts: 38.2 us -> 1.02 us  [the longest x1 0.72 us: on_device(): jnp.stack([factor[:, row, :, col, :] * keep[col, row][None, :, None] if k...]
    squeeze x0 -> x10, local copies, waits for them, and re-layouts: none -> 24.3 us  [the longest x9 13 us: mine(): return (both[0], both[1])]
    all_gather x5 -> x0, waiting for transfers between devices: 21.9 us -> none  [on_device(): lax.all_gather(masked[:, step + 1:, :, step, :], 'col', axis=3, tiled=True)]
    all_to_all x11 -> x5, local copies, waits for them, and re-layouts: 22.6 us -> 1.57 us  [the longest x3 1 us: on_device(): low = lax.all_to_all(share, 'core', split_axis=0, concat_axis=2, tiled=True)]
  transfers between devices with their start and end apart: 17 -> 4, of which waited for: 10 -> 3; matrix products, arithmetic and copies ran while one was open for 24% -> 32% of each run, Pallas kernels for 0% -> 35%
where the time goes in v1:
time: 538 us; the launch traced here: 532 us
  Pallas kernels  184 us (34%)
  matrix products  97 us (18%)
  waiting for transfers between devices  96.6 us (18%)
  local copies, waits for them, and re-layouts  92.6 us (17%)
  other arithmetic  32.6 us (6%)
  between operations  15.1 us (3%)
  starting transfers between devices  9.91 us (2%)
    pallas_call x1, Pallas kernels, gather_blocks(): pl.pallas_call(functools.partial(gather_kernel, nb), out_shape=jax.ShapeD...  184 us
    dot_general x40, matrix products, single(): lax.dot_general(a, b, (((contract,), (0,)), ((), ())), precision=lax.Prec...  97 us
    reduce_scatter x1, waiting for transfers between devices, on_device(): lax.psum_scatter(partial_sum, ('zh', 'a', 'b', 'zl'), scatter_dimension=0...  85 us
    slice x1, local copies, waits for them, and re-layouts, block(): both = full[where[kind, row, col]]  28.5 us
    unnamed x94, local copies, waits for them, and re-layouts  18.5 us
    squeeze x9, local copies, waits for them, and re-layouts, mine(): return (both[0], both[1])  13 us
    unnamed x18, other arithmetic  12.1 us
    sub x6, other arithmetic, on_device(): weight[0] * h[row][0] - weight[1] * h[row][1]  11.6 us
  transfers between devices with their start and end apart: 4, of which 3 were waited for; matrix products, arithmetic and copies ran while one was open for 32% of the time, Pallas kernels for 35%

profile of v1, /device:TPU:6, one launch (start us, length us, event | category | flops | bytes accessed | tf_op | source)
XLA Modules:
  0.0 532.0 jit_solution(5266846530380001162)
XLA Ops:
  9.6 4.4 copy.429
  30.6 184.3 %shard_map.46 = f32[21,2,512,512]{3,2,1,0:T(8,128)} custom-call(f32[21,2,256,128]{3,2,1,0:T(8,128)} %fusion.124.pack), custom_call_target="tpu_custom_call" | custom-call | tf_op jit(solution)/shard_map/pallas_call | solution.py:130
  214.9 28.5 %fusion.198 = (f32[1,2,512,512]{3,2,1,0:T(8,128)}, f32[1,2,512,512]{3,2,1,0:T(8,128)}, f32[1,2,512,512]{3,2,1,0:T(8,128)}, f32[1,2,512,512]{3,2,1,0:T(8,128)}, f...) fusion(f32[21,2,512,512]{3,2,1,0:T(8,128)} %shard_map.46), kind=kLoop, calls=%fused_computation.401 | loop fusion | bytes 79691776 | tf_op jit(solution)/shard_map/slice | solution.py:184
  243.5 4.7 fusion.199
  276.7 2.4 fusion.183
  279.1 2.4 fusion.189
  285.3 2.4 fusion.182
  294.0 2.4 fusion.46
  296.4 2.4 fusion.40
  302.7 2.7 fusion.42
  305.4 2.7 fusion.36
  315.9 2.4 fusion.54
  318.2 2.4 fusion.52
  320.6 2.4 fusion.50
  323.0 2.4 fusion.48
  325.8 3.1 fusion.44
  328.9 3.1 fusion.38
  333.7 11.3 %slice_bitcast_fusion.17 = (f32[512,512]{1,0:T(8,128)S(1)}, f32[512,512]{1,0:T(8,128)S(1)}, f32[512,512]{1,0:T(8,128)}, f32[512,512]{1,0:T(8,128)S(1)}, f32[512,...) fusion(f32[21,2,512,512]{3,2,1,0:T(8,128)} %shard_map.46), kind=kLoop, calls=%fused_computation.108 | loop fusion | bytes 37748736 | tf_op jit(solution)/shard_map/squeeze | solution.py:185
  372.7 4.5 fusion.16
  377.2 3.5 fusion.22
  382.9 3.6 fusion
  386.5 3.6 fusion.8
  391.9 4.9 fusion.98
  396.8 4.6 fusion.97
  402.9 2.7 fusion.101
  405.6 2.8 concatenate.250
  408.4 85.0 %reduce-scatter.2.cloned.1.call-done = f32[32,1344]{1,0:T(8,128)} async-done(((f32[512,1344]{1,0:T(8,128)}), f32[32,1344]{1,0:T(8,128)}) %reduce-scatter.2.cloned.1.call-update) | async-done | bytes 172048 | tf_op jit(solution)/shard_map/reduce_scatter | solution.py:219
  496.3 3.8 all_to_all.36
  500.1 3.3 all-to-all-start.1
  505.8 2.6 all-to-all-done.1
  510.1 4.7 collective-permute-start.1
  514.8 9.0 %collective-permute-done.1 = f32[15,128,16]{1,2,0:T(8,128)S(1)} collective-permute-done((f32[15,128,16]{1,2,0:T(8,128)S(1)}, f32[15,128,16]{1,2,0:T(8,128)S(1)}, u32[]{:S(2)}, u32[]{:S(2)}) %collective-permute-start.1) | collective-permute-done | bytes 122912 | tf_op jit(solution)/shard_map/ppermute | solution.py:237
  (208 shorter events, 112.2 us)
Async XLA Ops:
  6.5 486.9 %reduce-scatter.2.cloned.1.call-start = ((), (), s32[]{:S(2)}) async-start(), calls=%async_computation.3 | async-start | bytes 3063808 | tf_op jit(solution)/shard_map/reduce_scatter | solution.py:219
  6.5 354.2 %collective-permute-start = (f32[2]{0:T(128)}, f32[2]{0:T(128)S(1)}, u32[]{:S(2)}, u32[]{:S(2)}) collective-permute-start(f32[2]{0:T(128)} %bitcast.601), channel_id=1, source_target_pairs={{0,16},{4,24},{8,20},{12,28},{16,0},{20,8},{24,4},{28,12},{1,17},{... | collective-permute-start | bytes 32 | tf_op jit(solution)/shard_map/ppermute | solution.py:177
  9.6 4.4 copy-start
  363.2 3.2 copy-start.10
  363.2 3.2 copy-start.11
  363.2 3.2 copy-start.15
  363.2 3.2 copy-start.16
  366.4 1.9 copy-start.9
  370.3 2.3 copy-start.6
  370.3 2.3 copy-start.7
  370.3 2.3 copy-start.8
  370.3 2.3 copy-start.14
  370.3 2.3 copy-start.17
  372.6 4.6 copy-start.3
  372.6 4.6 copy-start.4
  372.6 4.6 copy-start.5
  372.7 4.6 copy-start.18
  380.8 2.1 copy-start.1
  380.8 2.1 copy-start.2
  380.8 2.1 copy-start.19
  380.8 2.1 copy-start.20
  380.8 2.0 copy-start.21
  380.8 2.0 copy-start.22
  386.5 3.6 copy-start.13
  396.8 4.6 copy-start.12
  500.1 8.3 %all-to-all-start.1 = ((f32[4,1,7680]{2,1,0:T(1,128)}), f32[4,1,7680]{2,1,0:T(1,128)S(1)}, u32[]{:S(2)}, u32[]{:S(2)}) async-start(f32[4,1,7680]{2,1,0:T(1,128)} %reshape.364), calls=%async_computation.2 | async-start | bytes 245760 | tf_op jit(solution)/shard_map/all_to_all | solution.py:224
  510.1 13.7 %collective-permute-start.1 = (f32[15,128,16]{1,2,0:T(8,128)S(1)}, f32[15,128,16]{1,2,0:T(8,128)S(1)}, u32[]{:S(2)}, u32[]{:S(2)}) collective-permute-start(f32[15,128,16]{1,2,0:T(8,128)S(1)} %all_to_all.33), channel_id=1, source_target_pairs={{0,0},{1,64},{2,4},{3,68},{4,2},{5,66},{6,6},{7,70},{8,32},{9,96},... | collective-permute-start | bytes 368648 | tf_op jit(solution)/shard_map/ppermute | solution.py:237
  524.0 0.7 copy-start.23
Sparse Core Ops, SparseCore 0:
  408.6 84.8 reduce-scatter.1

commit v2 on v1

v2 whole, which is shorter than its diff:
```python
import functools

import jax
import jax.numpy as jnp
from jax import lax
from jax.experimental import pallas as pl
from jax.experimental.pallas import tpu as pltpu
from jax.sharding import Mesh
from jax.sharding import PartitionSpec as P

AXES = ("a", "b", "zl", "core", "zh", "x")
MESH = pl.DeviceIdType.MESH


def block_order(nsup):
    lower = [("L", row, col) for col in range(1, nsup - 1) for row in range(col + 1, nsup)]
    diag = [("D", col, col) for col in range(nsup - 1, 0, -1)]
    first = [("L", row, 0) for row in range(1, nsup)]
    return lower + diag + first + [("D", 0, 0)]


def tri(row):
    return row * (row + 1) // 2


def split(value):
    high = value.astype(jnp.bfloat16)
    return high, (value - high.astype(jnp.float32)).astype(jnp.bfloat16)


def dot(a, b, dim):
    return lax.dot_general(a, b, (((1,), (dim,)), ((), ())), preferred_element_type=jnp.float32)


def window_kernel(
    nsup, pack, weight, full, out,
    blk, own_cols, flip, acc_z, acc_g, z_high, z_low, g_high, g_low, real, part1, sum1, part2,
    z_send, z_recv, x_send, x_recv, c_send, c_recv, r_send, r_recv, blk_sem, own_sem,
):
    order = block_order(nsup)
    where = {item: i for i, item in enumerate(order)}
    nb = len(order)
    last = nb - 1
    first0 = where[("L", 1, 0)]
    a_, b_, zl, core, zh, x = (lax.axis_index(n) for n in AXES)
    ncol = lax.axis_size("x")
    rows, cols = pack.shape[2], pack.shape[3]
    width = full.shape[2]
    half_w = width // 2
    n = cols // 2
    unit = 2 * n
    right, left, far = lax.rem(x + 1, ncol), lax.rem(x + ncol - 1, ncol), lax.rem(x + 2, ncol)
    to_z = {"zl": 1 - zl, "core": zh, "zh": core}
    to_right, to_left, to_core = {"x": right}, {"x": left}, {"core": 1 - core}

    def other(value, flag):
        return 1 - value if flag else value

    z_peers = [(other(zh, d >> 1), other(zl, d & 1)) for d in (1, 2, 3)]
    y_peers = [(other(a_, d >> 1), other(b_, d & 1)) for d in (1, 2, 3)]
    barrier = pltpu.get_barrier_semaphore()
    peers = [to_z, to_right, to_left, to_core]
    peers += [{"zh": h, "zl": l} for h, l in z_peers] + [{"a": p, "b": q} for p, q in y_peers]
    for peer in peers:
        pl.semaphore_signal(barrier, inc=1, device_id=peer, device_id_type=MESH)
    pl.semaphore_wait(barrier, len(peers))

    both, half0, half1 = pl.ds(0, 2), pl.ds(0, 1), pl.ds(1, 1)

    def tile(b, row, col, parts=both):
        return full.at[
            b,
            parts,
            pl.ds(pl.multiple_of(row * rows, rows), rows),
            pl.ds(pl.multiple_of(col * cols, cols), cols),
        ]

    def remote(src, dst, send, recv, peer):
        return pltpu.make_async_remote_copy(src, dst, send, recv, device_id=peer, device_id_type=MESH)

    def z_copy(b, row):
        return remote(pack.at[b], tile(b, row, x), z_send.at[b], z_recv.at[b], to_z)

    def x_copy(b, kind, col, parts, peer):
        ref = tile(b, core, col, parts)
        return remote(ref, ref, x_send.at[kind, b], x_recv.at[kind, b], peer)

    def c_copy(b, kind, col, parts, row):
        ref = tile(b, row, col, parts)
        return remote(ref, ref, c_send.at[kind, b], c_recv.at[kind, b], to_core)

    c_kinds = ((0, x, both), (1, left, both), (2, right, both), (3, far, half0), (4, far, half1))

    z_order, late = [0, 1], list(range(first0, nb))
    for b in range(2, first0):
        z_order.append(b)
        if late:
            z_order.append(late.pop(0))
    z_order += late
    for b in z_order:
        z_copy(b, zh).start()

    def own_part(b):
        z_copy(b, core).wait_recv()
        c_copy(b, 0, x, both, core).start()

    def own(b):
        if b < first0:
            own_part(b)
        x_copy(b, 0, x, both, to_right).start()
        x_copy(b, 1, x, both, to_left).start()

    def pass_on(b):
        x_copy(b, 0, left, both, to_right).wait_recv()
        x_copy(b, 2, left, half0, to_right).start()
        c_copy(b, 1, left, both, core).start()
        x_copy(b, 1, right, both, to_left).wait_recv()
        x_copy(b, 3, right, half1, to_left).start()
        c_copy(b, 2, right, both, core).start()

    def finish(b):
        x_copy(b, 2, far, half0, to_right).wait_recv()
        c_copy(b, 3, far, half0, core).start()
        x_copy(b, 3, far, half1, to_left).wait_recv()
        c_copy(b, 4, far, half1, core).start()

    def service(s):
        if s + 2 < last:
            own(s + 2)
        if 1 <= s and first0 + s - 1 <= last:
            own_part(first0 + s - 1)
        if s < last:
            pass_on(s)
        if 1 <= s <= last:
            finish(s - 1)

    def arrived(b):
        for kind, col, parts in c_kinds:
            if kind > 0 or b < first0:
                c_copy(b, kind, col, parts, 1 - core).wait_recv()

    def blk_copy(b, slot):
        return pltpu.make_async_copy(full.at[b], blk.at[slot], blk_sem.at[slot])

    def unit_rows(index):
        return pl.ds(pl.multiple_of(index * unit, unit), unit)

    def turned(q):
        flip[q] = jnp.transpose(own_cols[q])
        return flip[q, pl.ds(pl.multiple_of(core * n, n), n), :]

    def load_own(b):
        copy = pltpu.make_async_copy(
            full.at[b, :, :, pl.ds(pl.multiple_of(x * cols, cols), cols)], own_cols, own_sem
        )
        copy.start()
        copy.wait()

    def set_first(acc, index):
        for q in range(2):
            acc[0, pl.ds(index * unit + q * n, n), :] = turned(q)
        acc[1, pl.ds(index * unit, unit), :] = jnp.zeros((unit, width), jnp.float32)

    def begin():
        for row in range(1, nsup):
            c_copy(first0 + row - 1, 0, x, both, 1 - core).wait_recv()
            load_own(first0 + row - 1)
            set_first(acc_z, tri(row - 1))
        finish_z(1)

    def joined(acc, index):
        p, q = acc[0, unit_rows(index), :], acc[1, unit_rows(index), :]
        return p[:n] - q[n:], p[n:] + q[:n]

    def finish_z(row):
        @pl.loop(0, row)
        def _(k):
            re, im = joined(acc_z, tri(row - 1) + k)
            high, low = split(-jnp.concatenate([re, im], axis=0))
            z_high[unit_rows(tri(row) + k), :] = high
            z_low[unit_rows(tri(row) + k), :] = low

        lane = lax.broadcasted_iota(jnp.int32, (unit, width), 1)
        line = lax.broadcasted_iota(jnp.int32, (unit, width), 0)
        hit = (lane == line + x * cols + core * n) & (line < n)
        z_high[pl.ds((tri(row) + row) * unit, unit), :] = jnp.where(hit, 1.0, 0.0).astype(jnp.bfloat16)
        z_low[pl.ds((tri(row) + row) * unit, unit), :] = jnp.zeros((unit, width), jnp.bfloat16)

    def multiply(acc, acc_at, high, low, at, units, slot, transposed, fresh):
        m = units * unit
        here, there = pl.ds(at * unit, m), pl.ds(acc_at * unit, m)

        @pl.loop(0, 4)
        def _(i):
            q, piece = i // 2, pl.ds(pl.multiple_of((i % 2) * half_w, half_w), half_w)
            if transposed:
                right_high, right_low = split(blk[slot, q, piece, :])
                dim = 1
            else:
                right_high, right_low = split(blk[slot, q, :, piece])
                dim = 0
            total = dot(high[here, :], right_high, dim)
            total += dot(low[here, :], right_high, dim)
            total += dot(high[here, :], right_low, dim)
            if fresh:
                acc[q, there, piece] = total
            else:
                acc[q, there, piece] += total

    def forward(row, mid, slot):
        own_cols[...] = blk[slot, :, :, pl.ds(pl.multiple_of(x * cols, cols), cols)]
        set_first(acc_z, tri(row - 1) + mid)
        multiply(acc_z, tri(row - 1), z_high, z_low, tri(mid), mid, slot, True, False)
        if row == nsup - 1:
            finish_z(mid + 1)

    def backward(row, low_row, slot):
        if low_row == row:
            multiply(acc_g, 0, z_high, z_low, tri(row), row + 1, slot, False, True)
        else:
            multiply(acc_g, 0, g_high, g_low, tri(low_row), row + 1, slot, False, False)
        if low_row == nsup - 1:
            finish_g(row)

    def finish_g(row):
        w_re, w_im = weight[0], weight[1]

        @pl.loop(0, row + 1)
        def _(k):
            re, im = joined(acc_g, k)
            real[tri(row) + k] = (w_re * re - w_im * im).reshape(real.shape[1:])
            if row > 0:
                high, low = split(-jnp.concatenate([re, im], axis=0))
                g_high[unit_rows(tri(row) + k), :] = high
                g_low[unit_rows(tri(row) + k), :] = low

        for copy in first_stage(row):
            copy.start()

    def first_stage(row):
        span = pl.ds(tri(row), row + 1)
        copies = []
        for d, (h, l) in enumerate(z_peers):
            lanes = pl.ds(pl.multiple_of(h * half_w, half_w), half_w)
            copies.append(
                remote(
                    real.at[span, :, l, :, lanes], part1.at[d, span], r_send.at[0, row, d], r_recv.at[0, row, d],
                    {"zh": h, "zl": l},
                )
            )
        return copies

    def second_stage(row):
        span = pl.ds(tri(row), row + 1)
        copies = []
        for d, (p, q) in enumerate(y_peers):
            lanes = pl.ds(pl.multiple_of(p * cols, cols), cols)
            copies.append(
                remote(
                    sum1.at[span, q, :, lanes], part2.at[d, span], r_send.at[1, row, d], r_recv.at[1, row, d],
                    {"a": p, "b": q},
                )
            )
        return copies

    def reduce_first(row):
        for copy in first_stage(row):
            copy.wait_recv()
        span = pl.ds(tri(row), row + 1)
        lanes = pl.ds(pl.multiple_of(zh * half_w, half_w), half_w)
        sum1[span] = real[span, :, zl, :, lanes] + part1[0, span] + part1[1, span] + part1[2, span]
        for copy in second_stage(row):
            copy.start()

    def reduce_second(row):
        for copy in second_stage(row):
            copy.wait_recv()
        span = pl.ds(tri(row), row + 1)
        lanes = pl.ds(pl.multiple_of(a_ * cols, cols), cols)
        out[span] = sum1[span, b_, :, lanes] + part2[0, span] + part2[1, span] + part2[2, span]

    items = []
    for b in range(nsup * (nsup - 1) // 2 - (nsup - 1)):
        kind, row, mid = order[b]
        items.append((functools.partial(forward, row, mid), b, b, mid))
    for row in range(nsup - 1, 0, -1):
        items.append((functools.partial(backward, row, row), where[("D", row, row)], where[("D", row, row)], row + 1))
        for low_row in range(row + 1, nsup):
            items.append(
                (functools.partial(backward, row, low_row), where[("L", low_row, row)], where[("D", row, row)], row + 1)
            )
    for low_row in range(1, nsup):
        b = where[("L", low_row, 0)]
        items.append((functools.partial(backward, 0, low_row), b, b, 1))

    own(0)
    own(1)
    state = {"done": -1, "loaded": -1}
    seen = set()

    def fetch(i):
        if i <= state["loaded"] or i >= len(items) or items[i][2] + 1 > state["done"]:
            return
        b = items[i][1]
        if b not in seen:
            seen.add(b)
            arrived(b)
        blk_copy(b, i % 2).start()
        state["loaded"] = i

    todo, started, summed = 0, [], []
    ready_at = first0 - where[("L", 1, 0)] + nsup + 1
    finals = {}
    for i, (fn, b, avail, units) in enumerate(items):
        if fn.func is backward and fn.args[1] == nsup - 1:
            finals[i] = fn.args[0]
    for s in range(last + 1):
        service(s)
        state["done"] = s
        if s == ready_at:
            begin()
        if s < ready_at:
            continue
        for row in summed:
            reduce_second(row)
        summed = list(started)
        for row in started:
            reduce_first(row)
        started = []
        budget = 6 if s < last else 10**6
        while todo < len(items) and items[todo][2] + 1 <= s and budget > 0:
            fetch(todo)
            fetch(todo + 1)
            blk_copy(items[todo][1], todo % 2).wait()
            if todo == len(items) - nsup + 1:
                c_copy(last, 0, x, both, 1 - core).wait_recv()
                load_own(last)
                set_first(acc_g, 0)
            items[todo][0](todo % 2)
            budget -= items[todo][3]
            if todo in finals:
                started.append(finals[todo])
            todo += 1
    for row in summed:
        reduce_second(row)
    for row in started:
        reduce_first(row)
    for row in started:
        reduce_second(row)

    for b in range(nb):
        z_copy(b, zh).wait_send()
        c_copy(b, 0, x, both, core).wait_send()
        if b < last:
            x_copy(b, 0, x, both, to_right).wait_send()
            x_copy(b, 1, x, both, to_left).wait_send()
            x_copy(b, 2, left, half0, to_right).wait_send()
            x_copy(b, 3, right, half1, to_left).wait_send()
            for kind, col, parts in c_kinds[1:]:
                c_copy(b, kind, col, parts, core).wait_send()
    for row in range(nsup):
        for copy in first_stage(row) + second_stage(row):
            copy.wait_send()


def window_share(pack, weight, nsup, ncol):
    nb, parts, rows, cols = pack.shape
    width, unit, pairs = 2 * rows, cols, tri(nsup)
    sems = pltpu.SemaphoreType.DMA
    f32, bf16 = jnp.float32, jnp.bfloat16
    return pl.pallas_call(
        functools.partial(window_kernel, nsup),
        out_shape=(
            jax.ShapeDtypeStruct((nb, parts, width, width), f32),
            jax.ShapeDtypeStruct((pairs, 16, cols), f32),
        ),
        in_specs=[pl.BlockSpec(memory_space=pl.ANY), pl.BlockSpec(memory_space=pltpu.SMEM)],
        out_specs=(pl.BlockSpec(memory_space=pl.ANY), pl.BlockSpec(memory_space=pltpu.VMEM)),
        scratch_shapes=[
            pltpu.VMEM((2, parts, width, width), f32),
            pltpu.VMEM((parts, width, cols), f32),
            pltpu.VMEM((parts, cols, width), f32),
            pltpu.VMEM((2, tri(nsup - 1) * unit, width), f32),
            pltpu.VMEM((2, nsup * unit, width), f32),
            pltpu.VMEM((pairs * unit, width), bf16),
            pltpu.VMEM((pairs * unit, width), bf16),
            pltpu.VMEM((pairs * unit, width), bf16),
            pltpu.VMEM((pairs * unit, width), bf16),
            pltpu.VMEM((pairs, 2, 2, 16, width), f32),
            pltpu.VMEM((3, pairs, 2, 16, width // 2), f32),
            pltpu.VMEM((pairs, 2, 16, width // 2), f32),
            pltpu.VMEM((3, pairs, 16, cols), f32),
            sems((nb,)), sems((nb,)), sems((4, nb)), sems((4, nb)), sems((5, nb)), sems((5, nb)),
            sems((2, nsup, 3)), sems((2, nsup, 3)), sems((2,)), sems,
        ],
        compiler_params=pltpu.CompilerParams(
            collective_id=0, has_side_effects=True, vmem_limit_bytes=60 * 1024 * 1024
        ),
    )(pack, weight)[1]


def on_device(l_factor, dinv, weights, tiles):
    zh = lax.axis_index("zh")
    ncol = lax.axis_size("x")
    factor, diag_inv = l_factor[0], dinv[0]
    nsup, rows = factor.shape[1], factor.shape[2]
    width = 2 * rows
    tile_rows = nsup * width // tiles.shape[1]
    expanded = jnp.repeat(tiles.reshape(nsup, nsup, -1), tile_rows, axis=2)
    keep = lax.dynamic_slice_in_dim(expanded, zh * rows, rows, 2).astype(jnp.float32)
    pack = jnp.stack(
        [
            factor[:, row, :, col, :] * keep[col, row][None, :, None] if kind == "L" else diag_inv[:, row]
            for kind, row, col in block_order(nsup)
        ]
    )
    perm = [((l * 2 + k) * 2 + h, ((1 - l) * 2 + h) * 2 + k) for l in range(2) for k in range(2) for h in range(2)]
    weight = lax.ppermute(weights[0], ("zl", "core", "zh"), perm)
    share = window_share(pack, weight, nsup, ncol)

    pairs = [(row, col) for row in range(nsup) for col in range(row + 1)]
    turned = jnp.swapaxes(share, 1, 2)
    low = lax.all_to_all(turned, ("b", "zl", "core"), split_axis=1, concat_axis=2, tiled=True)
    low = low.reshape(*low.shape[:2], 2, 2, 2, 16)
    low = jnp.transpose(low, (0, 1, 4, 2, 3, 5)).reshape(*low.shape[:2], -1)
    off = jnp.stack([share[i] for i, (row, col) in enumerate(pairs) if row > col], axis=0)
    jumps = []
    for a in range(2):
        for b in range(2):
            for l in range(2):
                for k in range(2):
                    for h in range(2):
                        for c in range(ncol):
                            src = ((((a * 2 + b) * 2 + l) * 2 + k) * 2 + h) * ncol + c
                            d = (c % 2, k, b, l, c // 2, h * 2 + a)
                            dst = ((((d[0] * 2 + d[1]) * 2 + d[2]) * 2 + d[3]) * 2 + d[4]) * ncol + d[5]
                            jumps.append((src, dst))
    mirrored = lax.ppermute(off, AXES, jumps)

    spot = {pair: i for i, pair in enumerate(pairs)}
    offs = {pair: i for i, pair in enumerate(p for p in pairs if p[0] > p[1])}
    grid = [
        jnp.stack([low[spot[(row, col)]] if row >= col else mirrored[offs[(col, row)]] for col in range(nsup)], axis=1)
        for row in range(nsup)
    ]
    return jnp.stack(grid)[:, None]


def solution(mesh):
    fine = Mesh(mesh.devices.reshape(2, 2, 2, 2, 2, 4), AXES)
    pole = ("a", "b", "zl", "core")
    return jax.shard_map(
        on_device,
        mesh=fine,
        in_specs=(P(pole, None, None, "zh", None, "x"), P(pole, None, None, "zh", "x"), P(pole, None), P()),
        out_specs=P(None, "zh", pole, None, "x"),
        check_vma=False,
    )
```

time: 538 us -> 347 us (0.64)
  matrix products: 97 us -> 0 us
  waiting for transfers between devices: 96.6 us -> 0.01 us
  Pallas kernels: 184 us -> 238 us
  other arithmetic: 32.6 us -> 2.51 us
  between operations: 15.1 us -> 0.41 us
    dot_general x40 -> x0, matrix products: 97 us -> none  [single(): lax.dot_general(a, b, (((contract,), (0,)), ((), ())), precision=lax.Prec...]
    reduce_scatter x1 -> x0, waiting for transfers between devices: 85 us -> none  [on_device(): lax.psum_scatter(partial_sum, ('zh', 'a', 'b', 'zl'), scatter_dimension=0...]
    pallas_call x1, Pallas kernels: 184 us -> 238 us  [window_share(): pl.pallas_call(functools.partial(window_kernel, nsup), out_shape=(jax.Sha...]
    squeeze x10 -> x0, local copies, waits for them, and re-layouts: 24.3 us -> none  [the longest x9 13 us: mine(): return (both[0], both[1])]
    sub x14 -> x0, other arithmetic: 16.8 us -> none  [the longest x6 11.6 us: on_device(): weight[0] * h[row][0] - weight[1] * h[row][1]]
    unnamed x94 -> x51, local copies, waits for them, and re-layouts: 18.5 us -> 30.1 us
    unnamed x18 -> x15, other arithmetic: 12.1 us -> 1.45 us
    another operation x4 -> x24, local copies, waits for them, and re-layouts: 0.3 us -> 9.61 us  [the longest x23 8.23 us: on_device(): jnp.stack([low[spot[row, col]] if row >= col else mirrored[offs[col, row]...]
  transfers between devices with their start and end apart: 4 -> 3, of which waited for: 3 -> 0; matrix products, arithmetic and copies ran while one was open for 32% -> 24% of each run, Pallas kernels for 35% -> 0%
where the time goes in v2:
time: 347 us; the launch traced here: 343 us
  Pallas kernels  238 us (69%)
  local copies, waits for them, and re-layouts  92.1 us (27%)
  starting transfers between devices  9.92 us (3%)
    pallas_call x1, Pallas kernels, window_share(): pl.pallas_call(functools.partial(window_kernel, nsup), out_shape=(jax.Sha...  238 us
    slice x23, local copies, waits for them, and re-layouts, on_device(): low[spot[row, col]]  50 us
    unnamed x51, local copies, waits for them, and re-layouts  30.1 us
    another operation x23, local copies, waits for them, and re-layouts, on_device(): jnp.stack([low[spot[row, col]] if row >= col else mirrored[offs[col, row]...  8.23 us
  transfers between devices with their start and end apart: 3, of which 0 were waited for; matrix products, arithmetic and copies ran while one was open for 24% of the time, Pallas kernels for 0%

profile of v2, /device:TPU:6, one launch (start us, length us, event | category | flops | bytes accessed | tf_op | source)
XLA Modules:
  0.0 343.1 jit_solution(2383728277346554291)
XLA Ops:
  0.0 1.9 collective-permute-start
  3.0 4.4 %copy.97 = f32[1,2,6,256,6,128]{5,3,1,4,2,0:T(8,128)S(1)} copy(f32[1,2,6,256,6,128]{5,3,4,2,1,0:T(8,128)} %param.4) | data formatting | bytes 18874368 | tf_op args[0]
  9.3 2.4 copy-done
  12.2 238.2 %shard_map.46 = (f32[21,2,512,512]{3,2,1,0:T(8,128)}, f32[21,16,128]{2,1,0:T(8,128)}) custom-call(f32[21,2,256,128]{3,2,1,0:T(8,128)} %copy-done, f32[2]{0:T(128)} %copy-done.3), custom_call_target="tpu_custom_call" | custom-call | tf_op jit(solution)/shard_map/pallas_call | solution.py:371
  251.7 1.4 copy.68
  253.2 1.5 reshape.221
  254.7 3.4 all-to-all-start
  258.1 1.3 constant_dynamic-update-slice_fusion.3
  259.4 1.3 constant_dynamic-update-slice_fusion.2
  260.8 1.4 constant_dynamic-update-slice_fusion.1
  262.1 1.4 constant_dynamic-update-slice_fusion
  263.5 4.6 %collective-permute-start.1 = (f32[15,16,128]{2,1,0:T(8,128)}, f32[15,16,128]{2,1,0:T(8,128)S(1)}, u32[]{:S(2)}, u32[]{:S(2)}) collective-permute-start(f32[15,16,128]{2,1,0:T(8,128)} %constant_dynamic-update-slice_fusion), channel_id=1, source_target_pairs={{0,0},{1,64},{2,4},{3,68},{4,2},{5,66},{6,6},{7,70},{8,32},{9,96},... | collective-permute-start | bytes 368648 | tf_op jit(solution)/shard_map/ppermute | solution.py:438
  270.9 8.6 %fusion.36 = (f32[1,16,2,2,2,16]{0,5,2,4,3,1:T(8,128)S(1)}, f32[1,16,2,2,2,16]{0,5,2,4,3,1:T(8,128)S(1)}, f32[1,16,2,2,2,16]{0,5,2,4,3,1:T(8,128)}, f32[1,16,2,2...) fusion(f32[21,16,2,2,2,16]{0,5,2,4,3,1:T(8,128)S(1)} %bitcast.222), kind=kLoop, calls=%fused_computation.122 | loop fusion | bytes 311296 | tf_op jit(solution)/shard_map/slice | solution.py:443
  279.5 1.7 fusion.37
  281.1 2.1 copy.86
  283.4 2.1 copy.71
  285.6 2.1 copy.73
  287.8 2.1 copy.72
  290.0 2.1 copy.74
  292.2 2.1 copy.75
  294.4 2.1 copy.76
  296.6 2.1 copy.77
  300.7 2.1 copy.78
  303.5 2.1 copy.79
  306.3 2.1 copy.80
  309.1 2.1 copy.81
  313.2 2.1 copy.82
  316.0 2.1 copy.83
  318.8 2.1 copy.84
  329.3 2.1 copy.87
  331.5 2.1 copy.88
  333.7 2.1 copy.89
  (99 shorter events, 32.0 us)
Async XLA Ops:
  0.0 11.7 %collective-permute-start = (f32[2]{0:T(128)}, f32[2]{0:T(128)S(1)}, u32[]{:S(2)}, u32[]{:S(2)}) collective-permute-start(f32[2]{0:T(128)} %bitcast.264), channel_id=1, source_target_pairs={{0,16},{4,24},{8,20},{12,28},{16,0},{20,8},{24,4},{28,12},{1,17},{... | collective-permute-start | bytes 32 | tf_op jit(solution)/shard_map/ppermute | solution.py:418
  3.0 4.4 %copy-start.1 = (f32[1,2,6,256,128]{4,3,2,1,0:T(8,128)S(1)}, f32[1,2,6,256,128]{4,3,2,1,0:T(8,128)}, u32[]{:S(2)}) copy-start(f32[1,2,6,256,128]{4,3,2,1,0:T(8,128)} %param.5) | copy-start | bytes 4718596
  9.3 2.4 copy-start
  11.7 0.5 copy-start.3
  254.7 13.4 %all-to-all-start = ((f32[8,1,5376]{2,1,0:T(1,128)}), f32[8,1,5376]{2,1,0:T(1,128)S(1)}, u32[]{:S(2)}, u32[]{:S(2)}) async-start(f32[8,1,5376]{2,1,0:T(1,128)} %reshape.221), calls=%async_computation | async-start | bytes 344064 | tf_op jit(solution)/shard_map/all_to_all | solution.py:423
  263.5 76.0 %collective-permute-start.1 = (f32[15,16,128]{2,1,0:T(8,128)}, f32[15,16,128]{2,1,0:T(8,128)S(1)}, u32[]{:S(2)}, u32[]{:S(2)}) collective-permute-start(f32[15,16,128]{2,1,0:T(8,128)} %constant_dynamic-update-slice_fusion), channel_id=1, source_target_pairs={{0,0},{1,64},{2,4},{3,68},{4,2},{5,66},{6,6},{7,70},{8,32},{9,96},... | collective-permute-start | bytes 368648 | tf_op jit(solution)/shard_map/ppermute | solution.py:438
  342.4 0.7 copy-start.2

commit v3 on v2

--- a/solution.py
+++ b/solution.py
@@ -23,6 +23,10 @@
     return row * (row + 1) // 2
 
 
+def off(nsup, row):
+    return tri(nsup) - tri(row + 1)
+
+
 def split(value):
     high = value.astype(jnp.bfloat16)
     return high, (value - high.astype(jnp.float32)).astype(jnp.bfloat16)
@@ -34,8 +38,10 @@
 
 def window_kernel(
     nsup, pack, weight, full, out,
-    blk, own_cols, flip, acc_z, acc_g, z_high, z_low, g_high, g_low, real, part1, sum1, part2,
-    z_send, z_recv, x_send, x_recv, c_send, c_recv, r_send, r_recv, blk_sem, own_sem,
+    weigh, blk, own_cols, acc_z, acc_g, z_high, z_low, g_high, g_low, real, part1, sum1, part2, share, mirror,
+    low_from, low_to,
+    z_send, z_recv, x_send, x_recv, c_send, c_recv, r_send, r_recv, m_send, m_recv, l_send, l_recv, w_sems,
+    blk_sem, own_sem,
 ):
     order = block_order(nsup)
     where = {item: i for i, item in enumerate(order)}
@@ -61,8 +67,17 @@
     barrier = pltpu.get_barrier_semaphore()
     peers = [to_z, to_right, to_left, to_core]
     peers += [{"zh": h, "zl": l} for h, l in z_peers] + [{"a": p, "b": q} for p, q in y_peers]
+    l_peers = [(other(b_, d >> 2), other(zl, (d >> 1) & 1), other(core, d & 1)) for d in range(1, 8)]
+    peers += [{"b": i, "zl": j, "core": k} for i, j, k in l_peers]
+    place = 4 * b_ + 2 * zl + core
+    goes_to = (lax.rem(x, 2), core, b_, zl, x // 2, zh * 2 + a_)
+    comes_from = (lax.rem(x, 2), zl, core, b_, x // 2, zh * 2 + a_)
+    stays = (a_ == goes_to[0]) & (b_ == core) & (zl == b_) & (zh == goes_to[4]) & (x == goes_to[5])
+    moves = jnp.logical_not(stays)
+    peers += [dict(zip(AXES, goes_to)), dict(zip(AXES, comes_from))]
     for peer in peers:
         pl.semaphore_signal(barrier, inc=1, device_id=peer, device_id_type=MESH)
+
     pl.semaphore_wait(barrier, len(peers))
 
     both, half0, half1 = pl.ds(0, 2), pl.ds(0, 1), pl.ds(1, 1)
@@ -97,6 +112,8 @@
         if late:
             z_order.append(late.pop(0))
     z_order += late
+    w_copy = remote(weight, weigh, w_sems.at[0], w_sems.at[1], to_z)
+    w_copy.start()
     for b in z_order:
         z_copy(b, zh).start()
 
@@ -124,9 +141,11 @@
         x_copy(b, 3, far, half1, to_left).wait_recv()
         c_copy(b, 4, far, half1, core).start()
 
+    ahead = 4
+
     def service(s):
-        if s + 2 < last:
-            own(s + 2)
+        if s + ahead < last:
+            own(s + ahead)
         if 1 <= s and first0 + s - 1 <= last:
             own_part(first0 + s - 1)
         if s < last:
@@ -145,27 +164,27 @@
     def unit_rows(index):
         return pl.ds(pl.multiple_of(index * unit, unit), unit)
 
-    def turned(q):
-        flip[q] = jnp.transpose(own_cols[q])
-        return flip[q, pl.ds(pl.multiple_of(core * n, n), n), :]
-
-    def load_own(b):
-        copy = pltpu.make_async_copy(
-            full.at[b, :, :, pl.ds(pl.multiple_of(x * cols, cols), cols)], own_cols, own_sem
-        )
-        copy.start()
-        copy.wait()
-
-    def set_first(acc, index):
+    def own_copy(i):
+        columns = pl.ds(pl.multiple_of(x * cols, cols), cols)
+        return pltpu.make_async_copy(full.at[first0 + i, :, :, columns], own_cols.at[i], own_sem.at[i])
+
+    def set_first(acc, index, i):
+        lane = lax.broadcasted_iota(jnp.int32, (n, cols), 1)
+        line = lax.broadcasted_iota(jnp.int32, (n, cols), 0)
+        pick = jnp.where(lane == line + core * n, 1.0, 0.0).astype(jnp.bfloat16)
         for q in range(2):
-            acc[0, pl.ds(index * unit + q * n, n), :] = turned(q)
+            high, low = split(own_cols[i, q])
+            acc[0, pl.ds(index * unit + q * n, n), :] = dot(pick, high, 1) + dot(pick, low, 1)
         acc[1, pl.ds(index * unit, unit), :] = jnp.zeros((unit, width), jnp.float32)
 
     def begin():
+        for i in range(nsup):
+            c_copy(first0 + i, 0, x, both, 1 - core).wait_recv()
+            own_copy(i).start()
+        for i in range(nsup):
+            own_copy(i).wait()
         for row in range(1, nsup):
-            c_copy(first0 + row - 1, 0, x, both, 1 - core).wait_recv()
-            load_own(first0 + row - 1)
-            set_first(acc_z, tri(row - 1))
+            set_first(acc_z, tri(row - 1), row - 1)
         finish_z(1)
 
     def joined(acc, index):
@@ -187,48 +206,39 @@
         z_low[pl.ds((tri(row) + row) * unit, unit), :] = jnp.zeros((unit, width), jnp.bfloat16)
 
     def multiply(acc, acc_at, high, low, at, units, slot, transposed, fresh):
-        m = units * unit
-        here, there = pl.ds(at * unit, m), pl.ds(acc_at * unit, m)
-
-        @pl.loop(0, 4)
-        def _(i):
-            q, piece = i // 2, pl.ds(pl.multiple_of((i % 2) * half_w, half_w), half_w)
-            if transposed:
-                right_high, right_low = split(blk[slot, q, piece, :])
-                dim = 1
-            else:
-                right_high, right_low = split(blk[slot, q, :, piece])
-                dim = 0
-            total = dot(high[here, :], right_high, dim)
-            total += dot(low[here, :], right_high, dim)
-            total += dot(high[here, :], right_low, dim)
+        m, kept = units * unit, (units - fresh) * unit
+        here = pl.ds(at * unit, m)
+
+        @pl.loop(0, 2)
+        def _(q):
+            right_high, right_low = split(blk[slot, q])
+            dim = 1 if transposed else 0
+            upper = high[here, :]
+            total = dot(jnp.concatenate([upper, low[here, :]], axis=0), right_high, dim)
+            total = total[:m] + total[m:] + dot(upper, right_low, dim)
+            if kept:
+                acc[q, pl.ds(acc_at * unit, kept), :] += total[:kept]
             if fresh:
-                acc[q, there, piece] = total
-            else:
-                acc[q, there, piece] += total
+                acc[q, pl.ds(acc_at * unit + kept, fresh * unit), :] = total[kept:]
 
     def forward(row, mid, slot):
-        own_cols[...] = blk[slot, :, :, pl.ds(pl.multiple_of(x * cols, cols), cols)]
-        set_first(acc_z, tri(row - 1) + mid)
-        multiply(acc_z, tri(row - 1), z_high, z_low, tri(mid), mid, slot, True, False)
+        multiply(acc_z, tri(row - 1), z_high, z_low, tri(mid), mid + 1, slot, True, 1)
         if row == nsup - 1:
             finish_z(mid + 1)
 
     def backward(row, low_row, slot):
         if low_row == row:
-            multiply(acc_g, 0, z_high, z_low, tri(row), row + 1, slot, False, True)
+            multiply(acc_g, 0, z_high, z_low, tri(row), row + 1, slot, False, row + 1)
         else:
-            multiply(acc_g, 0, g_high, g_low, tri(low_row), row + 1, slot, False, False)
-        if low_row == nsup - 1:
-            finish_g(row)
+            multiply(acc_g, 0, g_high, g_low, tri(low_row), row + 1, slot, False, 0)
 
     def finish_g(row):
-        w_re, w_im = weight[0], weight[1]
+        w_re, w_im = weigh[0:1, :], weigh[1:2, :]
 
         @pl.loop(0, row + 1)
         def _(k):
             re, im = joined(acc_g, k)
-            real[tri(row) + k] = (w_re * re - w_im * im).reshape(real.shape[1:])
+            real[off(nsup, row) + k] = (w_re * re - w_im * im).reshape(real.shape[1:])
             if row > 0:
                 high, low = split(-jnp.concatenate([re, im], axis=0))
                 g_high[unit_rows(tri(row) + k), :] = high
@@ -238,7 +248,7 @@
             copy.start()
 
     def first_stage(row):
-        span = pl.ds(tri(row), row + 1)
+        span = pl.ds(off(nsup, row), row + 1)
         copies = []
         for d, (h, l) in enumerate(z_peers):
             lanes = pl.ds(pl.multiple_of(h * half_w, half_w), half_w)
@@ -251,7 +261,7 @@
         return copies
 
     def second_stage(row):
-        span = pl.ds(tri(row), row + 1)
+        span = pl.ds(off(nsup, row), row + 1)
         copies = []
         for d, (p, q) in enumerate(y_peers):
             lanes = pl.ds(pl.multiple_of(p * cols, cols), cols)
@@ -266,7 +276,7 @@
     def reduce_first(row):
         for copy in first_stage(row):
             copy.wait_recv()
-        span = pl.ds(tri(row), row + 1)
+        span = pl.ds(off(nsup, row), row + 1)
         lanes = pl.ds(pl.multiple_of(zh * half_w, half_w), half_w)
         sum1[span] = real[span, :, zl, :, lanes] + part1[0, span] + part1[1, span] + part1[2, span]
         for copy in second_stage(row):
@@ -275,9 +285,70 @@
     def reduce_second(row):
         for copy in second_stage(row):
             copy.wait_recv()
-        span = pl.ds(tri(row), row + 1)
+        span = pl.ds(off(nsup, row), row + 1)
         lanes = pl.ds(pl.multiple_of(a_ * cols, cols), cols)
-        out[span] = sum1[span, b_, :, lanes] + part2[0, span] + part2[1, span] + part2[2, span]
+        share[span] = sum1[span, b_, :, lanes] + part2[0, span] + part2[1, span] + part2[2, span]
+        if row > 0:
+
+            @pl.when(moves)
+            def _():
+                mirror_copy(row).start()
+
+        if row == 2:
+            start_low(0)
+            start_low(1)
+        if row == 0:
+            start_low(2)
+
+    def mirror_copy(row):
+        span = pl.ds(off(nsup, row), row)
+        return remote(
+            share.at[span], mirror.at[span], m_send.at[row], m_recv.at[row], dict(zip(AXES, goes_to))
+        )
+
+    def low_copies(g):
+        copies = []
+        for d, (i, j, k) in enumerate(l_peers):
+            lines = pl.ds(pl.multiple_of((4 * i + 2 * j + k) * 16, 16), 16)
+            copies.append(
+                remote(
+                    low_from.at[g, lines], low_to.at[g, place], l_send.at[g, d], l_recv.at[g, d],
+                    {"b": i, "zl": j, "core": k},
+                )
+            )
+        return copies
+
+    def start_low(g):
+        low_from[g] = jnp.transpose(share[pl.ds(8 * g, 8)].reshape(cols, cols))
+        low_to[g, place] = low_from[g, pl.ds(pl.multiple_of(place * 16, 16), 16), :]
+        for copy in low_copies(g):
+            copy.start()
+
+    def finish_low(g):
+        for copy in low_copies(g):
+            copy.wait_recv()
+        places = [4 * j + 2 * k + i for i in range(2) for j in range(2) for k in range(2)]
+        for row in range(nsup):
+            for col in range(row + 1):
+                p = off(nsup, row) + col - 8 * g
+                if 0 <= p < 8:
+                    pieces = [low_to[g, s, :, p * 16 : p * 16 + 16] for s in places]
+                    out[row, col] = jnp.concatenate(pieces, axis=1)
+
+    def finish_mirror():
+        @pl.when(moves)
+        def _():
+            for row in range(1, nsup):
+                mirror_copy(row).wait_recv()
+
+        @pl.when(stays)
+        def _():
+            mirror[...] = share[pl.ds(0, tri(nsup))]
+
+        for row in range(1, nsup):
+            for col in range(row):
+                out[col, row] = mirror[off(nsup, row) + col]
+
 
     items = []
     for b in range(nsup * (nsup - 1) // 2 - (nsup - 1)):
@@ -293,8 +364,10 @@
         b = where[("L", low_row, 0)]
         items.append((functools.partial(backward, 0, low_row), b, b, 1))
 
-    own(0)
-    own(1)
+    for i in range(24 - tri(nsup)):
+        share[tri(nsup) + i] = jnp.zeros(share.shape[1:], jnp.float32)
+    for b in range(ahead):
+        own(b)
     state = {"done": -1, "loaded": -1}
     seen = set()
 
@@ -333,12 +406,13 @@
             fetch(todo + 1)
             blk_copy(items[todo][1], todo % 2).wait()
             if todo == len(items) - nsup + 1:
-                c_copy(last, 0, x, both, 1 - core).wait_recv()
-                load_own(last)
-                set_first(acc_g, 0)
+                set_first(acc_g, 0, nsup - 1)
             items[todo][0](todo % 2)
             budget -= items[todo][3]
             if todo in finals:
+                if finals[todo] == nsup - 1:
+                    w_copy.wait_recv()
+                finish_g(finals[todo])
                 started.append(finals[todo])
             todo += 1
     for row in summed:
@@ -347,6 +421,19 @@
         reduce_first(row)
     for row in started:
         reduce_second(row)
+    for g in range(3):
+        finish_low(g)
+    finish_mirror()
+
+    w_copy.wait_send()
+    for g in range(3):
+        for copy in low_copies(g):
+            copy.wait_send()
+
+    @pl.when(moves)
+    def _():
+        for row in range(1, nsup):
+            mirror_copy(row).wait_send()
 
     for b in range(nb):
         z_copy(b, zh).wait_send()
@@ -372,14 +459,14 @@
         functools.partial(window_kernel, nsup),
         out_shape=(
             jax.ShapeDtypeStruct((nb, parts, width, width), f32),
-            jax.ShapeDtypeStruct((pairs, 16, cols), f32),
+            jax.ShapeDtypeStruct((nsup, nsup, 16, cols), f32),
         ),
-        in_specs=[pl.BlockSpec(memory_space=pl.ANY), pl.BlockSpec(memory_space=pltpu.SMEM)],
+        in_specs=[pl.BlockSpec(memory_space=pl.ANY), pl.BlockSpec(memory_space=pltpu.VMEM)],
         out_specs=(pl.BlockSpec(memory_space=pl.ANY), pl.BlockSpec(memory_space=pltpu.VMEM)),
         scratch_shapes=[
+            pltpu.VMEM(weight.shape, f32),
             pltpu.VMEM((2, parts, width, width), f32),
-            pltpu.VMEM((parts, width, cols), f32),
-            pltpu.VMEM((parts, cols, width), f32),
+            pltpu.VMEM((nsup, parts, width, cols), f32),
             pltpu.VMEM((2, tri(nsup - 1) * unit, width), f32),
             pltpu.VMEM((2, nsup * unit, width), f32),
             pltpu.VMEM((pairs * unit, width), bf16),
@@ -390,8 +477,13 @@
             pltpu.VMEM((3, pairs, 2, 16, width // 2), f32),
             pltpu.VMEM((pairs, 2, 16, width // 2), f32),
             pltpu.VMEM((3, pairs, 16, cols), f32),
+            pltpu.VMEM((24, 16, cols), f32),
+            pltpu.VMEM((pairs, 16, cols), f32),
+            pltpu.VMEM((3, cols, cols), f32),
+            pltpu.VMEM((3, 8, 16, cols), f32),
             sems((nb,)), sems((nb,)), sems((4, nb)), sems((4, nb)), sems((5, nb)), sems((5, nb)),
-            sems((2, nsup, 3)), sems((2, nsup, 3)), sems((2,)), sems,
+            sems((2, nsup, 3)), sems((2, nsup, 3)), sems((nsup,)), sems((nsup,)), sems((3, 7)), sems((3, 7)), sems((2,)),
+            sems((2,)), sems((nsup,)),
         ],
         compiler_params=pltpu.CompilerParams(
             collective_id=0, has_side_effects=True, vmem_limit_bytes=60 * 1024 * 1024
@@ -414,36 +506,9 @@
             for kind, row, col in block_order(nsup)
         ]
     )
-    perm = [((l * 2 + k) * 2 + h, ((1 - l) * 2 + h) * 2 + k) for l in range(2) for k in range(2) for h in range(2)]
-    weight = lax.ppermute(weights[0], ("zl", "core", "zh"), perm)
-    share = window_share(pack, weight, nsup, ncol)
-
-    pairs = [(row, col) for row in range(nsup) for col in range(row + 1)]
-    turned = jnp.swapaxes(share, 1, 2)
-    low = lax.all_to_all(turned, ("b", "zl", "core"), split_axis=1, concat_axis=2, tiled=True)
-    low = low.reshape(*low.shape[:2], 2, 2, 2, 16)
-    low = jnp.transpose(low, (0, 1, 4, 2, 3, 5)).reshape(*low.shape[:2], -1)
-    off = jnp.stack([share[i] for i, (row, col) in enumerate(pairs) if row > col], axis=0)
-    jumps = []
-    for a in range(2):
-        for b in range(2):
-            for l in range(2):
-                for k in range(2):
-                    for h in range(2):
-                        for c in range(ncol):
-                            src = ((((a * 2 + b) * 2 + l) * 2 + k) * 2 + h) * ncol + c
-                            d = (c % 2, k, b, l, c // 2, h * 2 + a)
-                            dst = ((((d[0] * 2 + d[1]) * 2 + d[2]) * 2 + d[3]) * 2 + d[4]) * ncol + d[5]
-                            jumps.append((src, dst))
-    mirrored = lax.ppermute(off, AXES, jumps)
-
-    spot = {pair: i for i, pair in enumerate(pairs)}
-    offs = {pair: i for i, pair in enumerate(p for p in pairs if p[0] > p[1])}
-    grid = [
-        jnp.stack([low[spot[(row, col)]] if row >= col else mirrored[offs[(col, row)]] for col in range(nsup)], axis=1)
-        for row in range(nsup)
-    ]
-    return jnp.stack(grid)[:, None]
+    weight = jnp.broadcast_to(jnp.pad(weights[0], (0, 6))[:, None], (8, width))
+    blocks = window_share(pack, weight, nsup, ncol)
+    return jnp.transpose(blocks, (0, 2, 1, 3))[:, None]
 
 
 def solution(mesh):

time: 347 us -> 271 us (0.78)
  local copies, waits for them, and re-layouts: 92.1 us -> 14.2 us
  starting transfers between devices: 9.92 us -> 0 us
  other arithmetic: 2.51 us -> 12.1 us
  Pallas kernels: 238 us -> 243 us
    slice x23 -> x0, local copies, waits for them, and re-layouts: 50 us -> none  [on_device(): low[spot[row, col]]]
    unnamed x51 -> x9, local copies, waits for them, and re-layouts: 30.1 us -> 11.9 us
    unnamed x15, other arithmetic: 1.45 us -> 12.1 us
    another operation x25 -> x0, local copies, waits for them, and re-layouts: 9.62 us -> none  [the longest x23 8.23 us: on_device(): jnp.stack([low[spot[row, col]] if row >= col else mirrored[offs[col, row]...]
    ppermute x2 -> x0, starting transfers between devices: 6.53 us -> none  [the longest x1 4.61 us: on_device(): mirrored = lax.ppermute(off, AXES, jumps)]
    pallas_call x1, Pallas kernels: 238 us -> 243 us  [window_share(): pl.pallas_call(functools.partial(window_kernel, nsup), out_shape=(jax.Sha...]
  transfers between devices with their start and end apart: 3 -> 0, of which waited for: 0 -> 0; matrix products, arithmetic and copies ran while one was open for 24% -> 0% of each run, Pallas kernels for 0% -> 0%
where the time goes in v3:
time: 271 us; the launch traced here: 270 us
  Pallas kernels  243 us (90%)
  local copies, waits for them, and re-layouts  14.2 us (5%)
  other arithmetic  12.1 us (4%)
    pallas_call x1, Pallas kernels, window_share(): pl.pallas_call(functools.partial(window_kernel, nsup), out_shape=(jax.Sha...  243 us
    unnamed x15, other arithmetic  12.1 us
    unnamed x9, local copies, waits for them, and re-layouts  11.9 us

profile of v3, /device:TPU:6, one launch (start us, length us, event | category | flops | bytes accessed | tf_op | source)
XLA Modules:
  0.0 269.7 jit_solution(6125538185757928525)
XLA Ops:
  0.0 0.7 pad.4
  0.7 0.8 copy.9
  1.4 0.1 copy.10
  1.6 0.7 broadcast_in_dim.13.weight
  2.2 0.1 broadcast_in_dim.12
  2.4 1.5 copy.16
  3.9 4.3 %copy.15 = f32[1,2,6,256,6,128]{5,3,1,4,2,0:T(8,128)S(1)} copy(f32[1,2,6,256,6,128]{5,3,4,2,1,0:T(8,128)} %param.4) | data formatting | bytes 18874368 | tf_op args[0]
  8.3 0.8 fusion.35
  9.1 0.8 fusion.33
  9.9 0.8 fusion.31
  10.7 0.8 fusion.29
  11.5 0.8 fusion.27
  12.3 0.8 fusion.25
  13.1 0.8 fusion.23
  13.9 0.8 fusion.21
  14.7 0.8 fusion.19
  15.5 0.8 fusion.17
  16.3 0.7 fusion.15
  17.0 0.7 fusion.14
  17.7 0.7 fusion.13
  18.5 0.7 fusion.12
  19.2 0.7 fusion.11
  19.9 0.8 fusion.10
  20.7 0.8 fusion.8
  21.5 0.8 fusion.6
  22.3 0.8 fusion.4
  23.1 0.8 fusion.2
  24.0 0.7 fusion.pack
  24.7 243.3 %shard_map.46 = (f32[21,2,512,512]{3,2,1,0:T(8,128)}, f32[6,6,16,128]{3,2,1,0:T(8,128)}) custom-call(f32[21,2,256,128]{3,2,1,0:T(8,128)} %fusion.pack, f32[8,512]{1,0:T(8,128)} %broadcast_in_dim.13.weight), custom_call_target="tpu_custom_call" | custom-call | tf_op jit(solution)/shard_map/pallas_call | solution.py:458
  268.0 1.7 copy.38
  (3 shorter events, 0.1 us)

commit v4 on v3

--- a/solution.py
+++ b/solution.py
@@ -37,11 +37,11 @@
 
 
 def window_kernel(
-    nsup, pack, weight, full, out,
-    weigh, blk, own_cols, acc_z, acc_g, z_high, z_low, g_high, g_low, real, part1, sum1, part2, share, mirror,
+    nsup, factor, dinv, tiles, weight, full, out,
+    pack, weigh, blk, own_cols, acc_z, acc_g, z_high, z_low, g_high, g_low, real, part1, sum1, part2, share, mirror,
     low_from, low_to,
     z_send, z_recv, x_send, x_recv, c_send, c_recv, r_send, r_recv, m_send, m_recv, l_send, l_recv, w_sems,
-    blk_sem, own_sem,
+    blk_sem, own_sem, pack_sem,
 ):
     order = block_order(nsup)
     where = {item: i for i, item in enumerate(order)}
@@ -114,7 +114,31 @@
     z_order += late
     w_copy = remote(weight, weigh, w_sems.at[0], w_sems.at[1], to_z)
     w_copy.start()
+
+    def pack_copy(b):
+        kind, row, col = order[b]
+        source = factor.at[0, :, row, :, col, :] if kind == "L" else dinv.at[0, :, row]
+        return pltpu.make_async_copy(source, pack.at[b], pack_sem.at[b])
+
+    def masked(b):
+        kind, row, col = order[b]
+        if kind == "L":
+            per_block = tiles.shape[1] // nsup
+            here = per_block // 2
+            size = rows // here
+
+            @pl.loop(0, 2 * here)
+            def _(i):
+                q, t = i // here, lax.rem(i, here)
+                keep = tiles[col, row * per_block + zh * here + t].astype(jnp.float32)
+                lines = pl.ds(pl.multiple_of(t * size, size), size)
+                pack[b, q, lines, :] = pack[b, q, lines, :] * keep
+
     for b in z_order:
+        pack_copy(b).start()
+    for b in z_order:
+        pack_copy(b).wait()
+        masked(b)
         z_copy(b, zh).start()
 
     def own_part(b):
@@ -141,7 +165,7 @@
         x_copy(b, 3, far, half1, to_left).wait_recv()
         c_copy(b, 4, far, half1, core).start()
 
-    ahead = 4
+    ahead, delay, pace = 2, 3, 8
 
     def service(s):
         if s + ahead < last:
@@ -150,8 +174,8 @@
             own_part(first0 + s - 1)
         if s < last:
             pass_on(s)
-        if 1 <= s <= last:
-            finish(s - 1)
+        if ahead <= s < last + ahead:
+            finish(s - ahead)
 
     def arrived(b):
         for kind, col, parts in c_kinds:
@@ -372,7 +396,7 @@
     seen = set()
 
     def fetch(i):
-        if i <= state["loaded"] or i >= len(items) or items[i][2] + 1 > state["done"]:
+        if i <= state["loaded"] or i >= len(items) or items[i][2] + ahead > state["done"]:
             return
         b = items[i][1]
         if b not in seen:
@@ -387,21 +411,24 @@
     for i, (fn, b, avail, units) in enumerate(items):
         if fn.func is backward and fn.args[1] == nsup - 1:
             finals[i] = fn.args[0]
-    for s in range(last + 1):
+    for s in range(last + ahead):
         service(s)
         state["done"] = s
         if s == ready_at:
             begin()
         if s < ready_at:
             continue
-        for row in summed:
-            reduce_second(row)
-        summed = list(started)
-        for row in started:
-            reduce_first(row)
-        started = []
-        budget = 6 if s < last else 10**6
-        while todo < len(items) and items[todo][2] + 1 <= s and budget > 0:
+        for row, since in list(summed):
+            if s >= since + delay:
+                reduce_second(row)
+                summed.remove((row, since))
+        for row, since in list(started):
+            if s >= since + delay:
+                reduce_first(row)
+                started.remove((row, since))
+                summed.append((row, s))
+        budget = pace if s < last + ahead - 1 else 10**6
+        while todo < len(items) and items[todo][2] + ahead <= s and budget > 0:
             fetch(todo)
             fetch(todo + 1)
             blk_copy(items[todo][1], todo % 2).wait()
@@ -413,13 +440,11 @@
                 if finals[todo] == nsup - 1:
                     w_copy.wait_recv()
                 finish_g(finals[todo])
-                started.append(finals[todo])
+                started.append((finals[todo], s))
             todo += 1
-    for row in summed:
-        reduce_second(row)
-    for row in started:
+    for row, since in started:
         reduce_first(row)
-    for row in started:
+    for row, since in summed + started:
         reduce_second(row)
     for g in range(3):
         finish_low(g)
@@ -450,8 +475,9 @@
             copy.wait_send()
 
 
-def window_share(pack, weight, nsup, ncol):
-    nb, parts, rows, cols = pack.shape
+def window_share(factor, dinv, tiles, weight, ncol):
+    _, parts, nsup, rows, _, cols = factor.shape
+    nb = tri(nsup)
     width, unit, pairs = 2 * rows, cols, tri(nsup)
     sems = pltpu.SemaphoreType.DMA
     f32, bf16 = jnp.float32, jnp.bfloat16
@@ -461,9 +487,15 @@
             jax.ShapeDtypeStruct((nb, parts, width, width), f32),
             jax.ShapeDtypeStruct((nsup, nsup, 16, cols), f32),
         ),
-        in_specs=[pl.BlockSpec(memory_space=pl.ANY), pl.BlockSpec(memory_space=pltpu.VMEM)],
+        in_specs=[
+            pl.BlockSpec(memory_space=pl.ANY),
+            pl.BlockSpec(memory_space=pl.ANY),
+            pl.BlockSpec(memory_space=pltpu.SMEM),
+            pl.BlockSpec(memory_space=pltpu.VMEM),
+        ],
         out_specs=(pl.BlockSpec(memory_space=pl.ANY), pl.BlockSpec(memory_space=pltpu.VMEM)),
         scratch_shapes=[
+            pltpu.VMEM((nb, parts, rows, cols), f32),
             pltpu.VMEM(weight.shape, f32),
             pltpu.VMEM((2, parts, width, width), f32),
             pltpu.VMEM((nsup, parts, width, cols), f32),
@@ -483,31 +515,18 @@
             pltpu.VMEM((3, 8, 16, cols), f32),
             sems((nb,)), sems((nb,)), sems((4, nb)), sems((4, nb)), sems((5, nb)), sems((5, nb)),
             sems((2, nsup, 3)), sems((2, nsup, 3)), sems((nsup,)), sems((nsup,)), sems((3, 7)), sems((3, 7)), sems((2,)),
-            sems((2,)), sems((nsup,)),
+            sems((2,)), sems((nsup,)), sems((nb,)),
         ],
         compiler_params=pltpu.CompilerParams(
             collective_id=0, has_side_effects=True, vmem_limit_bytes=60 * 1024 * 1024
         ),
-    )(pack, weight)[1]
+    )(factor, dinv, tiles, weight)[1]
 
 
 def on_device(l_factor, dinv, weights, tiles):
-    zh = lax.axis_index("zh")
-    ncol = lax.axis_size("x")
-    factor, diag_inv = l_factor[0], dinv[0]
-    nsup, rows = factor.shape[1], factor.shape[2]
-    width = 2 * rows
-    tile_rows = nsup * width // tiles.shape[1]
-    expanded = jnp.repeat(tiles.reshape(nsup, nsup, -1), tile_rows, axis=2)
-    keep = lax.dynamic_slice_in_dim(expanded, zh * rows, rows, 2).astype(jnp.float32)
-    pack = jnp.stack(
-        [
-            factor[:, row, :, col, :] * keep[col, row][None, :, None] if kind == "L" else diag_inv[:, row]
-            for kind, row, col in block_order(nsup)
-        ]
-    )
+    width = 2 * l_factor.shape[3]
     weight = jnp.broadcast_to(jnp.pad(weights[0], (0, 6))[:, None], (8, width))
-    blocks = window_share(pack, weight, nsup, ncol)
+    blocks = window_share(l_factor, dinv, tiles, weight, lax.axis_size("x"))
     return jnp.transpose(blocks, (0, 2, 1, 3))[:, None]
 
 

time: 271 us -> 227 us (0.84)
  Pallas kernels: 243 us -> 207 us
  other arithmetic: 12.1 us -> 0 us
  local copies, waits for them, and re-layouts: 14.2 us -> 17 us
    pallas_call x1, Pallas kernels: 243 us -> 207 us  [window_share(): pl.pallas_call(functools.partial(window_kernel, nsup), out_shape=(jax.Sha...]
    unnamed x15 -> x0, other arithmetic: 12.1 us -> none
    unnamed x9 -> x2, local copies, waits for them, and re-layouts: 11.9 us -> 15.7 us
where the time goes in v4:
time: 227 us; the launch traced here: 224 us
  Pallas kernels  207 us (91%)
  local copies, waits for them, and re-layouts  17 us (7%)
    pallas_call x1, Pallas kernels, window_share(): pl.pallas_call(functools.partial(window_kernel, nsup), out_shape=(jax.Sha...  207 us
    unnamed x2, local copies, waits for them, and re-layouts  15.7 us

profile of v4, /device:TPU:6, one launch (start us, length us, event | category | flops | bytes accessed | tf_op | source)
XLA Modules:
  0.0 224.2 jit_solution(17710484440006007989)
XLA Ops:
  0.0 0.7 pad.4
  0.7 0.7 broadcast_in_dim.4.weight
  1.3 14.0 %copy.5.factor = f32[1,2,6,256,6,128]{5,4,3,2,1,0:T(8,128)} copy(f32[1,2,6,256,6,128]{5,3,4,2,1,0:T(8,128)} %param.4) | data formatting | bytes 18874368 | tf_op args[0]
  15.3 207.1 %shard_map.46 = (f32[21,2,512,512]{3,2,1,0:T(8,128)}, f32[6,6,16,128]{3,2,1,0:T(8,128)}) custom-call(f32[1,2,6,256,6,128]{5,4,3,2,1,0:T(8,128)} %copy.5.factor, f32[1,2,6,256,128]{4,3,2,1,0:T(8,128)} %dinv.1, s32[6,24]{1,0:T(8,128)} %tiles.1, f32[8,512]{1,0:T(8,128)} %broadcast_in_dim.4.weight), custom_call_target="tpu_custom_call" | custom-call | tf_op jit(solution)/shard_map/pallas_call | solution.py:484
  222.5 1.7 copy.8

commit v5 on v4

--- a/solution.py
+++ b/solution.py
@@ -41,7 +41,7 @@
     pack, weigh, blk, own_cols, acc_z, acc_g, z_high, z_low, g_high, g_low, real, part1, sum1, part2, share, mirror,
     low_from, low_to,
     z_send, z_recv, x_send, x_recv, c_send, c_recv, r_send, r_recv, m_send, m_recv, l_send, l_recv, w_sems,
-    blk_sem, own_sem, pack_sem,
+    dx_send, dx_recv, dc_send, dc_recv, blk_sem, own_sem, pack_sem,
 ):
     order = block_order(nsup)
     where = {item: i for i, item in enumerate(order)}
@@ -117,7 +117,7 @@
 
     def pack_copy(b):
         kind, row, col = order[b]
-        source = factor.at[0, :, row, :, col, :] if kind == "L" else dinv.at[0, :, row]
+        source = factor.at[0, :, row, col] if kind == "L" else dinv.at[0, :, row]
         return pltpu.make_async_copy(source, pack.at[b], pack_sem.at[b])
 
     def masked(b):
@@ -165,19 +165,94 @@
         x_copy(b, 3, far, half1, to_left).wait_recv()
         c_copy(b, 4, far, half1, core).start()
 
-    ahead, delay, pace = 2, 3, 8
+    ahead, delay, pace = 2, 4, 5
+
+    sym0 = where[("D", nsup - 1, nsup - 1)]
+    syms = range(sym0, first0)
+
+    def piece(b, row, col, part=None, start=0, size=None):
+        return full.at[
+            b,
+            pl.ds(core if part is None else part, 1),
+            pl.ds(pl.multiple_of(row * cols + start, cols // 2), size or cols),
+            pl.ds(pl.multiple_of(col * cols, cols), cols),
+        ]
+
+    def dx_copy(b, kind, row, col, peer, start=0, size=None):
+        ref = piece(b, row, col, None, start, size)
+        return remote(ref, ref, dx_send.at[kind, b - sym0], dx_recv.at[kind, b - sym0], peer)
+
+    def dc_copy(b, kind, row, col, part, start=0, size=None):
+        ref = piece(b, row, col, part, start, size)
+        return remote(ref, ref, dc_send.at[kind, b - sym0], dc_recv.at[kind, b - sym0], to_core)
+
+    part_size = cols // 2
+    out_right = ((0, x), (1, far), (2, left))
+    out_left = ((3, x), (4, right))
+    in_left = ((0, left), (1, right), (2, far))
+    in_right = ((3, right), (4, far))
+    dc_kinds = (
+        (0, left, left, 0, cols), (1, right, left, 0, cols), (2, far, left, 0, cols),
+        (3, right, right, 0, cols), (4, far, right, 0, cols),
+        (5, far, far, 0, part_size), (6, far, far, part_size, part_size),
+    )
+
+    def own_sym(b):
+        c_copy(b, 0, x, both, 1 - core).wait_recv()
+        for kind, row in out_right:
+            dx_copy(b, kind, row, x, to_right).start()
+        for kind, row in out_left:
+            dx_copy(b, kind, row, x, to_left).start()
+
+    def pass_sym(b):
+        for kind, row in in_left:
+            dx_copy(b, kind, row, left, to_right).wait_recv()
+            if kind == 0:
+                dx_copy(b, 5, left, left, to_right, 0, part_size).start()
+            dc_copy(b, kind, row, left, core).start()
+        for kind, row in in_right:
+            dx_copy(b, kind, row, right, to_left).wait_recv()
+            if kind == 3:
+                dx_copy(b, 6, right, right, to_left, part_size, part_size).start()
+            dc_copy(b, kind, row, right, core).start()
+
+    def finish_sym(b):
+        dx_copy(b, 5, far, far, to_right, 0, part_size).wait_recv()
+        dc_copy(b, 5, far, far, core, 0, part_size).start()
+        dx_copy(b, 6, far, far, to_left, part_size, part_size).wait_recv()
+        dc_copy(b, 6, far, far, core, part_size, part_size).start()
+
+    def fill(slot):
+        def place_of(q, row, col):
+            return (
+                slot,
+                q,
+                pl.ds(pl.multiple_of(row * cols, cols), cols),
+                pl.ds(pl.multiple_of(col * cols, cols), cols),
+            )
+
+        @pl.loop(0, 2)
+        def _(q):
+            for row, col in ((left, x), (right, x), (far, x), (right, left), (far, left), (far, right)):
+                blk[place_of(q, col, row)] = jnp.transpose(blk[place_of(q, row, col)])
 
     def service(s):
+        if s + ahead + 2 in syms:
+            own_part(s + ahead + 2)
         if s + ahead < last:
-            own(s + ahead)
+            (own_sym if s + ahead in syms else own)(s + ahead)
         if 1 <= s and first0 + s - 1 <= last:
             own_part(first0 + s - 1)
         if s < last:
-            pass_on(s)
+            (pass_sym if s in syms else pass_on)(s)
         if ahead <= s < last + ahead:
-            finish(s - ahead)
+            (finish_sym if s - ahead in syms else finish)(s - ahead)
 
     def arrived(b):
+        if b in syms:
+            for kind, row, col, start, size in dc_kinds:
+                dc_copy(b, kind, row, col, 1 - core, start, size).wait_recv()
+            return
         for kind, col, parts in c_kinds:
             if kind > 0 or b < first0:
                 c_copy(b, kind, col, parts, 1 - core).wait_recv()
@@ -252,6 +327,7 @@
 
     def backward(row, low_row, slot):
         if low_row == row:
+            fill(slot)
             multiply(acc_g, 0, z_high, z_low, tri(row), row + 1, slot, False, row + 1)
         else:
             multiply(acc_g, 0, g_high, g_low, tri(low_row), row + 1, slot, False, 0)
@@ -463,7 +539,14 @@
     for b in range(nb):
         z_copy(b, zh).wait_send()
         c_copy(b, 0, x, both, core).wait_send()
-        if b < last:
+        if b in syms:
+            for kind, row in out_right + out_left:
+                dx_copy(b, kind, row, x, to_right).wait_send()
+            dx_copy(b, 5, left, left, to_right, 0, part_size).wait_send()
+            dx_copy(b, 6, right, right, to_left, part_size, part_size).wait_send()
+            for kind, row, col, start, size in dc_kinds:
+                dc_copy(b, kind, row, col, core, start, size).wait_send()
+        elif b < last:
             x_copy(b, 0, x, both, to_right).wait_send()
             x_copy(b, 1, x, both, to_left).wait_send()
             x_copy(b, 2, left, half0, to_right).wait_send()
@@ -476,7 +559,7 @@
 
 
 def window_share(factor, dinv, tiles, weight, ncol):
-    _, parts, nsup, rows, _, cols = factor.shape
+    _, parts, nsup, _, rows, cols = factor.shape
     nb = tri(nsup)
     width, unit, pairs = 2 * rows, cols, tri(nsup)
     sems = pltpu.SemaphoreType.DMA
@@ -515,7 +598,7 @@
             pltpu.VMEM((3, 8, 16, cols), f32),
             sems((nb,)), sems((nb,)), sems((4, nb)), sems((4, nb)), sems((5, nb)), sems((5, nb)),
             sems((2, nsup, 3)), sems((2, nsup, 3)), sems((nsup,)), sems((nsup,)), sems((3, 7)), sems((3, 7)), sems((2,)),
-            sems((2,)), sems((nsup,)), sems((nb,)),
+            *[sems((7, nsup - 1)) for _ in range(4)], sems((2,)), sems((nsup,)), sems((nb,)),
         ],
         compiler_params=pltpu.CompilerParams(
             collective_id=0, has_side_effects=True, vmem_limit_bytes=60 * 1024 * 1024
@@ -526,7 +609,8 @@
 def on_device(l_factor, dinv, weights, tiles):
     width = 2 * l_factor.shape[3]
     weight = jnp.broadcast_to(jnp.pad(weights[0], (0, 6))[:, None], (8, width))
-    blocks = window_share(l_factor, dinv, tiles, weight, lax.axis_size("x"))
+    factor = jnp.swapaxes(l_factor, 3, 4)
+    blocks = window_share(factor, dinv, tiles, weight, lax.axis_size("x"))
     return jnp.transpose(blocks, (0, 2, 1, 3))[:, None]
 
 

time: 227 us -> 202 us (0.89)
  local copies, waits for them, and re-layouts: 17 us -> 3.03 us
  Pallas kernels: 207 us -> 198 us
    unnamed x2 -> x1, local copies, waits for them, and re-layouts: 15.7 us -> 1.69 us
    pallas_call x1, Pallas kernels: 207 us -> 198 us  [window_share(): pl.pallas_call(functools.partial(window_kernel, nsup), out_shape=(jax.Sha...]
where the time goes in v5:
time: 202 us; the launch traced here: 201 us
  Pallas kernels  198 us (98%)
  local copies, waits for them, and re-layouts  3.03 us (2%)
    pallas_call x1, Pallas kernels, window_share(): pl.pallas_call(functools.partial(window_kernel, nsup), out_shape=(jax.Sha...  198 us

profile of v5, /device:TPU:6, one launch (start us, length us, event | category | flops | bytes accessed | tf_op | source)
XLA Modules:
  0.0 200.9 jit_solution(3954478947858432020)
XLA Ops:
  0.0 0.7 pad.4
  0.7 0.7 broadcast_in_dim.4.weight
  1.3 197.8 %shard_map.46 = (f32[21,2,512,512]{3,2,1,0:T(8,128)}, f32[6,6,16,128]{3,2,1,0:T(8,128)}) custom-call(f32[1,2,6,6,256,128]{5,4,3,2,1,0:T(8,128)} %bitcast.7, f32[1,2,6,256,128]{4,3,2,1,0:T(8,128)} %dinv.1, s32[6,24]{1,0:T(8,128)} %tiles.1, f32[8,512]{1,0:T(8,128)} %broadcast_in_dim.4.weight), custom_call_target="tpu_custom_call" | custom-call | tf_op jit(solution)/shard_map/pallas_call | solution.py:567
  199.2 1.7 copy.7

commit v6 on v5

--- a/solution.py
+++ b/solution.py
@@ -165,7 +165,7 @@
         x_copy(b, 3, far, half1, to_left).wait_recv()
         c_copy(b, 4, far, half1, core).start()
 
-    ahead, delay, pace = 2, 4, 5
+    ahead, delay, pace, early = 3, 4, 5, 12
 
     sym0 = where[("D", nsup - 1, nsup - 1)]
     syms = range(sym0, first0)
@@ -503,7 +503,7 @@
                 reduce_first(row)
                 started.remove((row, since))
                 summed.append((row, s))
-        budget = pace if s < last + ahead - 1 else 10**6
+        budget = 10**6 if s >= last + ahead - 1 else pace if s >= sym0 + ahead else early
         while todo < len(items) and items[todo][2] + ahead <= s and budget > 0:
             fetch(todo)
             fetch(todo + 1)
@@ -518,13 +518,19 @@
                 finish_g(finals[todo])
                 started.append((finals[todo], s))
             todo += 1
-    for row, since in started:
+    rest = [row for row, since in started if row > 0]
+    for row in rest:
         reduce_first(row)
-    for row, since in summed + started:
+    for row, since in summed:
         reduce_second(row)
-    for g in range(3):
-        finish_low(g)
+    reduce_first(0)
+    for row in rest:
+        reduce_second(row)
+    reduce_second(0)
+    finish_low(0)
+    finish_low(1)
     finish_mirror()
+    finish_low(2)
 
     w_copy.wait_send()
     for g in range(3):

time: 202 us -> 200 us (0.990)
  Pallas kernels: 198 us -> 194 us
    pallas_call x1, Pallas kernels: 198 us -> 194 us  [window_share(): pl.pallas_call(functools.partial(window_kernel, nsup), out_shape=(jax.Sha...]
where the time goes in v6:
time: 200 us; the launch traced here: 197 us
  Pallas kernels  194 us (97%)
  local copies, waits for them, and re-layouts  3.03 us (2%)
    pallas_call x1, Pallas kernels, window_share(): pl.pallas_call(functools.partial(window_kernel, nsup), out_shape=(jax.Sha...  194 us

profile of v6, /device:TPU:6, one launch (start us, length us, event | category | flops | bytes accessed | tf_op | source)
XLA Modules:
  0.0 197.0 jit_solution(6114268000857896133)
XLA Ops:
  0.0 0.7 pad.4
  0.7 0.7 broadcast_in_dim.4.weight
  1.3 193.9 %shard_map.46 = (f32[21,2,512,512]{3,2,1,0:T(8,128)}, f32[6,6,16,128]{3,2,1,0:T(8,128)}) custom-call(f32[1,2,6,6,256,128]{5,4,3,2,1,0:T(8,128)} %bitcast.7, f32[1,2,6,256,128]{4,3,2,1,0:T(8,128)} %dinv.1, s32[6,24]{1,0:T(8,128)} %tiles.1, f32[8,512]{1,0:T(8,128)} %broadcast_in_dim.4.weight), custom_call_target="tpu_custom_call" | custom-call | tf_op jit(solution)/shard_map/pallas_call | solution.py:573
  195.3 1.7 copy.7
